TPU v7x, 256 devices: a whole 4x4x8 slice. The times are simulated.
256 devices in a mesh: band: 16 (over y, z_lo, core), shard: 16 (over z_hi, x).
Axes of the slice: x: 4, y: 4, z: 8 (z_hi: 4, z_lo: 2; z = z_hi * 2 + z_lo), core: 2. Of those that a mesh axis runs over, the one named last changes fastest.
Arguments:
- activations: bfloat16 [1024, 2304], P('shard'), may hold values from -6 to 6
- encoder: bfloat16 [2304, 131072], P(None, ('band', 'shard')), may hold values from -0.125 to 0.125
- encoder_bias: float32 [131072], P(('band', 'shard')), may hold values from -1 to -0.25
- decoder: bfloat16 [131072, 2304], P(('band', 'shard')), may hold values from -0.125 to 0.125
Outputs:
- losses: float32 [16], replicated
- encoder_grad: bfloat16 [2304, 131072], P(None, ('band', 'shard'))
- decoder_grad: bfloat16 [131072, 2304], P(('band', 'shard'))
All inputs are finite; a program needn't handle non-finite values.
Results may differ from a plain program's by a relative error of at most 0.006.
Values may be sent and summed in bfloat16 or wider, within the bound.
No kernel may reach another device: no remote copies, remote signals or barrier semaphores. Data moves between devices by JAX's collectives and lax.ppermute only.
A program may use at most 128 MiB of HBM per device.

v0:
```python
import jax
import jax.numpy as jnp
from jax import lax
from jax.sharding import PartitionSpec as P


def over_pieces(value, axis):
    pieces = lax.all_gather(value, axis)
    return pieces.sum(axis=0)


def on_device(activations, encoder, encoder_bias, decoder):
    band_count = lax.axis_size("band")
    local_count = activations.shape[0]
    divisor = local_count * lax.axis_size("shard") * activations.shape[1]
    gathered = lax.all_gather(activations, "shard", axis=0, tiled=True)
    preact = jnp.dot(gathered, encoder, preferred_element_type=jnp.float32) + encoder_bias
    linear = jnp.maximum(preact, 0.0)
    active = (linear * linear).astype(jnp.bfloat16)
    act_rows = active
    band_part = lax.psum_scatter(
        jnp.dot(act_rows, decoder, preferred_element_type=jnp.float32),
        "shard",
        scatter_dimension=0,
        tiled=True,
    )
    local_rows = activations.astype(jnp.float32)
    stacked = lax.all_gather(band_part[None], "band", axis=0, tiled=True)
    prefix_recon = jnp.cumsum(stacked, axis=0)
    errors_all = local_rows[None] - prefix_recon
    losses = over_pieces(jnp.sum(errors_all * errors_all, axis=(1, 2)), "shard") / divisor
    tail_sums = jnp.flip(jnp.cumsum(jnp.flip(errors_all, 0), axis=0), 0)
    suffix = lax.dynamic_index_in_dim(tail_sums, lax.axis_index("band"), 0, keepdims=False)
    upstream = (-suffix / band_count).astype(jnp.bfloat16)
    shard_rows = lax.all_gather(upstream, "shard", axis=0, tiled=True)
    act_block = jnp.einsum("rd,ld->rl", shard_rows, decoder, preferred_element_type=jnp.float32)
    act_grads = act_block
    act_rows = active
    dec_grads = jnp.einsum("rl,rd->ld", act_rows, shard_rows, preferred_element_type=jnp.float32)
    act_grads, dec_grads = (act_grads, dec_grads)
    pre_grads = (2.0 * linear * act_grads).astype(jnp.bfloat16)
    encoder_grad = jnp.einsum(
        "rd,rl->dl", gathered, pre_grads, preferred_element_type=jnp.float32
    ).astype(jnp.bfloat16)
    return (losses, encoder_grad, dec_grads.astype(jnp.bfloat16))


def solution(mesh):
    return jax.shard_map(
        on_device,
        mesh=mesh,
        in_specs=(
            P("shard", None),
            P(None, ("band", "shard")),
            P(("band", "shard")),
            P(("band", "shard"), None),
        ),
        out_specs=(P(), P(None, ("band", "shard")), P(("band", "shard"), None)),
        check_vma=False,
    )
```

profile of v0, /device:TPU:35, one launch (start us, length us, event | category | flops | bytes accessed | tf_op | source)
XLA Modules:
  0.0 439.7 jit_solution(9953187625067713702)
XLA Ops:
  7.2 0.7 all-gather.7.cloned.1.call-update
  7.9 0.0 reduce-scatter.2.cloned.1.call-start
  8.0 87.1 %all-gather.7.cloned.1.call-done = bf16[1024,2304]{1,0:T(8,128)(2,1)} async-done(((bf16[64,2304]{1,0:T(8,128)(2,1)}), bf16[1024,2304]{1,0:T(8,128)(2,1)}) %all-gather.7.cloned.1.call-update) | async-done | bytes 4718608 | tf_op jit(solution)/shard_map/all_gather | solution.py:16
  95.1 5.2 %fusion.18 = f32[1024,512]{1,0:T(8,128)S(1)} fusion(bf16[1024,2304]{1,0:T(8,128)(2,1)} %all-gather.7.cloned.1.call-done, bf16[2304,512]{1,0:T(8,128)(2,1)} %param.5), kind=kOutput, calls=%fused_computation.20 | convolution fusion | flops 2415919104 | bytes 9175040 | tf_op jit(solution)/shard_map/dot_general | solution.py:17
  100.3 1.4 copy-done.4
  101.7 5.0 %fusion.12 = f32[1024,2304]{1,0:T(8,128)} fusion(bf16[512,2304]{1,0:T(8,128)(2,1)S(1)} %copy-done, f32[1024,512]{1,0:T(8,128)S(1)} %fusion.18, f32[512]{0:T(512)S(1)} %copy-done.2), kind=kOutput, calls=%fused_computation.13 | convolution fusion | flops 2418016256 | bytes 13895680 | tf_op jit(solution)/shard_map/dot_general | solution.py:22
  106.7 0.0 all-gather.9.cloned.1.call-start
  106.8 127.4 %reduce-scatter.2.cloned.1.call-done = f32[64,2304]{1,0:T(8,128)} async-done(((f32[1024,2304]{1,0:T(8,128)}), f32[64,2304]{1,0:T(8,128)}) %reduce-scatter.2.cloned.1.call-update) | async-done | bytes 589840 | tf_op jit(solution)/shard_map/reduce_scatter | solution.py:21
  234.2 0.0 all-gather.11.cloned.1.call-start
  234.3 61.3 %all-gather.9.cloned.1.call-done = f32[1024,2304]{1,0:T(8,128)} async-done(((f32[64,2304]{1,0:T(8,128)}), f32[1024,2304]{1,0:T(8,128)}) %all-gather.9.cloned.1.call-update) | async-done | bytes 9437200 | tf_op jit(solution)/shard_map/all_gather | solution.py:28
  295.6 7.3 %multiply_reduce_fusion = (f32[16]{0:T(128)S(1)}, f32[16,64,2304]{2,1,0:T(8,128)}) fusion(f32[16,64,2304]{2,1,0:T(8,128)} %bitcast.22, f32[64,2304]{1,0:T(8,128)S(1)} %convert_element_type.24), kind=kOutput, calls=%fused_computation | output fusion | flops 42467312 | bytes 19464256 | tf_op jit(solution)/shard_map/jit(cumsum)/reduce_window_sum | solution.py:29
  302.9 8.2 %rev.7 = f32[16,64,2304]{2,1,0:T(8,128)} reverse(f32[16,64,2304]{2,1,0:T(8,128)} %get-tuple-element.10), dimensions={0} | reverse | bytes 18874368 | tf_op jit(solution)/shard_map/jit(_flip)/rev | solution.py:32
  311.2 6.6 %fusion.17 = f32[16,64,2304]{2,1,0:T(8,128)} fusion(f32[16,64,2304]{2,1,0:T(8,128)} %rev.7), kind=kOutput, calls=%fused_computation.19 | output fusion | flops 35389440 | bytes 18874368 | tf_op jit(solution)/shard_map/jit(cumsum)/reduce_window_sum | solution.py:32
  317.8 8.2 %rev.8 = f32[16,64,2304]{2,1,0:T(8,128)} reverse(f32[16,64,2304]{2,1,0:T(8,128)} %fusion.17), dimensions={0} | reverse | bytes 18874368 | tf_op jit(solution)/shard_map/jit(_flip)/rev | solution.py:32
  326.0 1.8 multiply_convert_fusion.2
  327.9 0.6 dynamic-slice
  329.1 0.2 dynamic-update-slice
  329.4 33.6 %all-reduce = f32[256]{0:T(256)S(1)} all-reduce(f32[256]{0:T(256)S(1)} %dynamic-update-slice), channel_id=3, replica_groups=mesh['band'=16,'shard'=16] {'shard'}, use_global_device_ids=true, to_apply=%add | all-reduce | flops 256 | bytes 2048
  363.0 0.1 reshape.13
  363.1 0.5 broadcast_multiply_fusion
  363.6 47.0 %all-gather.11.cloned.1.call-done = bf16[1,1024,2304]{2,1,0:T(8,128)(2,1)} async-done(((bf16[1,64,2304]{2,1,0:T(8,128)(2,1)}), bf16[1,1024,2304]{2,1,0:T(8,128)(2,1)}) %all-gather.11.cloned.1.call-update) | async-done | bytes 4718608 | tf_op jit(solution)/shard_map/all_gather | solution.py:35
  410.6 11.2 %fusion.7 = bf16[2304,512]{0,1:T(8,128)(2,1)} fusion(bf16[1024,2304]{1,0:T(8,128)(2,1)} %all-gather.7.cloned.1.call-done, f32[1024,512]{1,0:T(8,128)} %copy-done.4, bf16[512,2304]{1,0:T(8,128)(2,1)S(1)} %copy-done, bf16[1,1024,2304]{2,1,0:T(8,128)(2,1)} %all-gather.11.cloned.1.call-done, f32[512]{0:T(512)S(1)} %copy-done.2), kind=kOutput, calls=%fused_computation.8 | convolution fusion | flops 4835639296 | bytes 16254976 | tf_op jit(solution)/shard_map/rd,rl->dl/dot_general | solution.py:42
  421.8 4.3 copy.8
  426.1 7.1 %fusion.4 = bf16[512,2304]{1,0:T(8,128)(2,1)} fusion(bf16[1,1024,2304]{2,1,0:T(8,128)(2,1)} %all-gather.11.cloned.1.call-done, f32[1024,512]{1,0:T(8,128)} %copy-done.4, f32[512]{0:T(512)S(1)} %copy-done.2), kind=kOutput, calls=%fused_computation.6 | convolution fusion | flops 2419195904 | bytes 9177088 | tf_op jit(solution)/shard_map/rl,rd->ld/dot_general | solution.py:39
  (16 shorter events, 0.2 us)
Async XLA Ops:
  7.2 94.5 %copy-start = (bf16[512,2304]{1,0:T(8,128)(2,1)S(1)}, bf16[512,2304]{1,0:T(8,128)(2,1)}, u32[]{:S(2)}) copy-start(bf16[512,2304]{1,0:T(8,128)(2,1)} %param.7) | copy-start | bytes 7077892
  7.2 87.9 %all-gather.7.cloned.1.call-start = ((), (), s32[]{:S(2)}) async-start(), calls=%async_computation.1 | async-start | bytes 5013504 | tf_op jit(solution)/shard_map/all_gather | solution.py:16
  7.9 93.7 %copy-start.2 = (f32[512]{0:T(512)S(1)}, f32[512]{0:T(512)}, u32[]{:S(2)}) copy-start(f32[512]{0:T(512)} %param.6) | copy-start | bytes 6148
  7.9 226.3 %reduce-scatter.2.cloned.1.call-start = ((), (), s32[]{:S(2)}) async-start(), calls=%async_computation.2 | async-start | bytes 10027008 | tf_op jit(solution)/shard_map/reduce_scatter | solution.py:21
  100.3 1.4 copy-start.4
  106.7 127.6 %copy-start.1 = (bf16[64,2304]{1,0:T(8,128)(2,1)S(1)}, bf16[64,2304]{1,0:T(8,128)(2,1)}, u32[]{:S(2)}) copy-start(bf16[64,2304]{1,0:T(8,128)(2,1)} %param.4) | copy-start | bytes 884740
  106.7 188.9 %all-gather.9.cloned.1.call-start = ((), (), s32[]{:S(2)}) async-start(), calls=%async_computation.3 | async-start | bytes 10027008 | tf_op jit(solution)/shard_map/all_gather | solution.py:28
  234.2 176.4 %all-gather.11.cloned.1.call-start = ((), (), s32[]{:S(2)}) async-start(), calls=%async_computation.4 | async-start | bytes 5013504 | tf_op jit(solution)/shard_map/all_gather | solution.py:35
  317.8 10.1 %copy-start.3 = (u32[256]{0:T(256)S(1)}, u32[256]{0:T(256)}, u32[]{:S(2)}) copy-start(u32[256]{0:T(256)} %constant.28) | copy-start | bytes 3076
Sparse Core Ops, SparseCore 0:
  10.4 84.6 all-gather.6
  106.8 127.2 reduce-scatter.1
  236.0 59.5 all-gather.8
  328.0 82.5 all-gather.10
where the time goes:
time: 440 us
  waiting for transfers between devices  324 us (74%)
  blocking collectives  33.6 us (8%)
  matrix products  28.5 us (6%)
  local copies, waits for them, and re-layouts  23.1 us (5%)
  other arithmetic  16.3 us (4%)
  between operations  14.5 us (3%)
    reduce_scatter x1, waiting for transfers between devices, on_device(): lax.psum_scatter(jnp.dot(act_rows, decoder, preferred_element_type=jnp.fl...  127 us
    all_gather x1, waiting for transfers between devices, on_device(): gathered = lax.all_gather(activations, 'shard', axis=0, tiled=True)  87.1 us
    all_gather x1, waiting for transfers between devices, on_device(): stacked = lax.all_gather(band_part[None], 'band', axis=0, tiled=True)  61.3 us
    all_gather x1, waiting for transfers between devices, on_device(): shard_rows = lax.all_gather(upstream, 'shard', axis=0, tiled=True)  47 us
    unnamed x1, blocking collectives  33.6 us
    rev x2, local copies, waits for them, and re-layouts, on_device(): tail_sums = jnp.flip(jnp.cumsum(jnp.flip(errors_all, 0), axis=0), 0)  16.5 us
    dot_general x1, matrix products, on_device(): jnp.einsum('rd,rl->dl', gathered, pre_grads, preferred_element_type=jnp.f...  11.2 us
  transfers between devices with their start and end apart: 4, of which 4 were waited for; matrix products, arithmetic and copies ran while one was open for 0% of the time, Pallas kernels for 0%

commit v1 on v0

v1 whole, which is shorter than its diff:
```python
import jax
import jax.numpy as jnp
from jax import lax
from jax.experimental import pallas as pl
from jax.experimental.pallas import tpu as pltpu
from jax.sharding import Mesh, PartitionSpec as P


BF = jnp.bfloat16
F32 = jnp.float32
NAMES = ("y", "zl", "core", "zh", "x")
BAND = ("y", "zl", "core")
SHARD = ("zh", "x")
N = 4
BANDS = 16
LANES = 128
DOWN = 1408
UP = 1536
Shape = jax.ShapeDtypeStruct


def spread(value, axis):
    return lax.all_to_all(jnp.broadcast_to(value[None], (N, *value.shape)), axis, 0, 0)


def pull(value, axis, step):
    return lax.ppermute(value, axis, [(i, (i - step) % N) for i in range(N)])


def gather_ring(value, axis):
    half = value.shape[0] // 2
    plus = pull(value, axis, 1)
    minus = pull(value, axis, -1)
    far_a = pull(plus[:half], axis, 1)
    far_b = pull(minus[half:], axis, -1)
    return value, plus, far_a, far_b, minus


def reduce_ring(blocks, axis):
    own, plus, two, minus = blocks
    half = own.shape[0] // 2
    far_a = pull(two[:half], axis, -1)
    far_b = pull(two[half:], axis, 1)
    plus = jnp.concatenate([(plus[:half].astype(F32) + far_a.astype(F32)).astype(BF), plus[half:]], 0)
    minus = jnp.concatenate([minus[:half], (minus[half:].astype(F32) + far_b.astype(F32)).astype(BF)], 0)
    plus = pull(plus, axis, -1)
    minus = pull(minus, axis, 1)
    return (own.astype(F32) + plus.astype(F32) + minus.astype(F32)).astype(BF)


def forward_kernel(
    at_ref, near_ref, near2_ref, far_ref, far2_ref, enc_ref, bias_ref, dec_ref, a_ref, linear_ref, active_ref, first_ref, second_ref
):
    half = near_ref.shape[1] // N

    def lay(mine, other):
        for z in range(N):
            a_ref[2 * half * z : 2 * half * z + half] = mine[0, half * z : half * z + half]
            a_ref[2 * half * z + half : 2 * half * z + 2 * half] = other[0, half * z : half * z + half]

    @pl.when(pl.program_id(0) != 2)
    def _():
        lay(near_ref, near2_ref)

    @pl.when(pl.program_id(0) == 2)
    def _():
        lay(far_ref, far2_ref)

    preact = jnp.dot(a_ref[...], enc_ref[...], preferred_element_type=F32) + bias_ref[...]
    linear = jnp.maximum(preact, 0.0)
    linear_ref[...] = linear
    active_ref[...] = (linear * linear).astype(BF)
    term = jnp.dot(active_ref[...], dec_ref[...], preferred_element_type=F32).astype(BF)
    for z in range(N):
        rows = slice(2 * half * z, 2 * half * z + 2 * half)
        place = pl.multiple_of(2 * half * ((at_ref[1] + z) % N), 2 * half)
        first_ref[0, pl.ds(place, 2 * half)] = term[rows, :DOWN]
        second_ref[z, 0] = term[rows, DOWN:]


def backward_kernel(
    at_ref, a0, a1, a2, a3, a4, b0, b1, b2, b3, b4, dec_ref, linear_ref, active_any, gathered_any,
    enc_out, dec_out, found_ref, up_ref, grad_ref, active_ref, gathered_ref, sems,
):
    block = a0.shape[0]
    rows = block // N
    width = up_ref.shape[1]
    rest = width - UP
    copies = [
        pltpu.make_async_copy(active_any, active_ref, sems.at[0]),
        pltpu.make_async_copy(gathered_any, gathered_ref, sems.at[1]),
    ]
    for copy in copies:
        copy.start()
    for x, pieces in enumerate(((a0,), (a1,), (a2, a3), (a4,))):
        z = 0
        for piece in pieces:
            for i in range(piece.shape[0] // rows):
                place = block * x + rows * ((z + N - at_ref[1]) % N)
                up_ref[pl.ds(pl.multiple_of(place, rows), rows), :UP] = piece[rows * i : rows * i + rows]
                z += 1
    found = jnp.zeros((8, LANES), F32)
    for z, pieces in enumerate(((b0,), (b1,), (b2, b3), (b4,))):
        x = 0
        for piece in pieces:
            for i in range(piece.shape[0] // rows):
                place = block * x + rows * z
                up_ref[place : place + rows, UP:] = piece[rows * i : rows * i + rows, :rest]
                found = found + piece[rows * i : rows * i + 8, rest:].astype(F32)
                x += 1
    found_ref[...] = found

    def first(x, _):
        span = pl.ds(pl.multiple_of(block * x, block), block)
        grads = lax.dot_general(up_ref[span], dec_ref[...], (((1,), (1,)), ((), ())), preferred_element_type=F32)
        grad_ref[span] = (2.0 * linear_ref[span] * grads).astype(BF)
        return 0

    lax.fori_loop(0, N, first, 0)
    contract = (((0,), (0,)), ((), ()))
    copies[0].wait()
    step = 2 * LANES

    def second(i, _):
        span = pl.ds(pl.multiple_of(step * i, step), step)
        dec_out[:, span] = lax.dot_general(
            active_ref[...], up_ref[:, span], contract, preferred_element_type=F32
        ).astype(BF)
        return 0

    lax.fori_loop(0, width // step, second, 0)
    copies[1].wait()

    def third(i, _):
        span = pl.ds(pl.multiple_of(step * i, step), step)
        enc_out[span] = lax.dot_general(
            gathered_ref[:, span], grad_ref[...], contract, preferred_element_type=F32
        ).astype(BF)
        return 0

    lax.fori_loop(0, width // step, third, 0)


def deal_kernel(core_ref, a_ref, b0, b1, b2, b3, dealt_ref):
    wide = dealt_ref.shape[2]
    cut = a_ref.shape[2] - wide
    part_a = jnp.sum(a_ref[...].astype(F32), axis=0).astype(dealt_ref.dtype)
    part_b = b0[...].astype(F32) + b1[...].astype(F32) + b2[...].astype(F32) + b3[...].astype(F32)
    part_b = part_b.astype(dealt_ref.dtype)
    flip = core_ref[0] * (BANDS // 4)
    for k in range(BANDS // 2):
        to = 2 * (k ^ flip)
        dealt_ref[to] = part_a[8 * k : 8 * k + 8, :wide]
        dealt_ref[to + 1, :, :cut] = part_a[8 * k : 8 * k + 8, wide:]
        dealt_ref[to + 1, :, cut:] = part_b[8 * k : 8 * k + 8]


def as_rows(found):
    high = found.astype(BF).astype(F32)
    low = found - high
    row = lax.broadcasted_iota(jnp.int32, (8, LANES), 0)
    return jnp.where(row == 0, high, jnp.where(row == 1, low, 0.0)).astype(BF)


def band_kernel(mixed_ref, local_ref, up_ref):
    wide = local_ref.shape[1]
    lane = lax.broadcasted_iota(jnp.int32, (1, LANES), 1)
    found = jnp.zeros((1, LANES), F32)
    error = local_ref[...].astype(F32)
    suffix = jnp.zeros_like(error)
    errors = []
    for k in range(BANDS):
        error = error - mixed_ref[k].astype(F32)
        errors.append(error)
        found = jnp.where(lane == k, jnp.sum(error * error), found)
    for k in reversed(range(BANDS)):
        suffix = suffix + errors[k]
        up_ref[k, :, :wide] = (suffix * (-1.0 / BANDS)).astype(BF)
    extra = as_rows(found)
    for k in range(BANDS):
        up_ref[k, :, wide:] = extra


def sort_kernel(core_ref, mixed_ref, up_a_ref, up_b_ref):
    wide = mixed_ref.shape[2] - LANES
    cut = UP - wide
    rest = 2 * wide - UP
    found = jnp.zeros((1, LANES), F32)
    flip = core_ref[0] * (BANDS // 4)
    up_b_ref[:, rest:] = jnp.zeros((up_b_ref.shape[0], LANES), BF)
    for k in range(BANDS // 2):
        rows = pl.ds(8 * k, 8)
        at = 2 * (k ^ flip)
        up_a_ref[rows, :wide] = mixed_ref[at, :, :wide]
        up_a_ref[rows, wide:] = mixed_ref[at + 1, :, :cut]
        up_b_ref[rows, :rest] = mixed_ref[at + 1, :, cut:wide]
    for k in range(BANDS):
        found = found + jnp.sum(mixed_ref[k, :, wide:].astype(F32), axis=0, keepdims=True)
    up_b_ref[:8, rest:] = as_rows(found)


SCALAR = pl.BlockSpec(memory_space=pltpu.SMEM)
LOCAL = pl.BlockSpec(memory_space=pltpu.VMEM)


def step(activations, encoder, encoder_bias, decoder):
    rows, width = activations.shape
    latents = encoder.shape[1]
    half = rows // 2
    block = rows * N
    total = block * N
    divisor = total * width
    rest = width - UP
    core = lax.axis_index("core")
    band = lax.axis_index(BAND)
    which = core.astype(jnp.int32).reshape(1)

    at = jnp.stack([lax.axis_index("x"), lax.axis_index("zh")]).astype(jnp.int32)

    column = jnp.concatenate(gather_ring(lax.dynamic_slice_in_dim(activations, core * half, half, 0), "zh"), 0)
    own, plus, far_a, far_b, minus = gather_ring(column, "x")
    near = jnp.stack([own, plus, minus])
    far = jnp.concatenate([far_a, far_b], 0)[None]
    near2, far2 = [lax.ppermute(v, "core", [(0, 1), (1, 0)]) for v in (near, far)]

    fixed = lambda i, at: (0, 0)
    by_row = lambda i, at: (i, 0)
    by_near = lambda i, at: ((i + 1) // 2, 0, 0)
    by_far = lambda i, at: (0, 0, 0)
    gathered, linear, active, first, second = pl.pallas_call(
        forward_kernel,
        grid_spec=pltpu.PrefetchScalarGridSpec(
            num_scalar_prefetch=1,
            grid=(N,),
            in_specs=[
                pl.BlockSpec((1, block // 2, width), by_near),
                pl.BlockSpec((1, block // 2, width), by_near),
                pl.BlockSpec((1, block // 2, width), by_far),
                pl.BlockSpec((1, block // 2, width), by_far),
                pl.BlockSpec((width, latents), fixed),
                pl.BlockSpec((1, latents), fixed),
                pl.BlockSpec((latents, width), fixed),
            ],
            out_specs=[
                pl.BlockSpec((block, width), by_row),
                pl.BlockSpec((block, latents), by_row),
                pl.BlockSpec((block, latents), by_row),
                pl.BlockSpec((1, block, DOWN), lambda i, at: (i, 0, 0)),
                pl.BlockSpec((N, 1, rows, width - DOWN), lambda i, at: (0, i, 0, 0)),
            ],
        ),
        out_shape=[
            Shape((total, width), BF),
            Shape((total, latents), F32),
            Shape((total, latents), BF),
            Shape((N, block, DOWN), BF),
            Shape((N, N, rows, width - DOWN), BF),
        ],
    )(at, near, near2, far, far2, encoder, encoder_bias.reshape(1, latents), decoder)

    first = reduce_ring(first, "x")
    second = reduce_ring(second.reshape(N, block, width - DOWN), "zh")
    first = lax.all_to_all(first.reshape(N, rows, DOWN), "zh", 0, 0)
    second = [second[o * rows : (o + 1) * rows] for o in range(N)]
    second = [second[0]] + [pull(second[o], "x", -o) for o in range(1, N)]

    wide = width // 2
    dealt = pl.pallas_call(
        deal_kernel,
        out_shape=Shape((BANDS, 8, wide), BF),
        in_specs=[SCALAR] + [LOCAL] * 5,
        out_specs=LOCAL,
    )(which, first, *second)
    mixed = lax.all_to_all(dealt, BAND, 0, 0)
    local = lax.dynamic_slice(activations, (8 * (band // 2), wide * (band % 2)), (8, wide))
    ups = pl.pallas_call(
        band_kernel,
        out_shape=Shape((BANDS, 8, wide + LANES), BF),
        in_specs=[LOCAL, LOCAL],
        out_specs=LOCAL,
    )(mixed, local)
    ups = lax.all_to_all(ups, BAND, 0, 0)
    up_a, up_b = pl.pallas_call(
        sort_kernel,
        out_shape=[Shape((rows, UP), BF), Shape((rows, rest + LANES), BF)],
        in_specs=[SCALAR, LOCAL],
        out_specs=[LOCAL, LOCAL],
    )(which, ups)

    others = [pull(up_b, "x", o) for o in range(1, N)]
    up_b = jnp.concatenate([up_b] + others, 0)
    up_a = spread(up_a, "zh")
    up_a = gather_ring(up_a.reshape(block, UP), "x")
    up_b = gather_ring(up_b, "zh")

    anywhere = pl.BlockSpec(memory_space=pl.ANY)
    enc_grads, dec_grads, found = pl.pallas_call(
        backward_kernel,
        in_specs=[SCALAR] + [LOCAL] * 12 + [anywhere] * 2,
        out_specs=[LOCAL] * 3,
        out_shape=[Shape((width, latents), BF), Shape((latents, width), BF), Shape((8, LANES), F32)],
        scratch_shapes=[
            pltpu.VMEM((total, width), BF),
            pltpu.VMEM((total, latents), BF),
            pltpu.VMEM((total, latents), BF),
            pltpu.VMEM((total, width), BF),
            pltpu.SemaphoreType.DMA((2,)),
        ],
    )(at, *up_a, *up_b, decoder, linear, active, gathered)
    losses = jnp.sum(found, axis=0)[:BANDS] / divisor
    return losses, enc_grads, dec_grads


def solution(mesh):
    grid = Mesh(mesh.devices.reshape(4, 2, 2, 4, 4), NAMES)
    both = BAND + SHARD
    return jax.shard_map(
        step,
        mesh=grid,
        in_specs=(P(SHARD, None), P(None, both), P(both), P(both, None)),
        out_specs=(P(), P(None, both), P(both, None)),
        check_vma=False,
    )
```

time: 440 us -> 269 us (0.61)
  the two profiles are of different devices: /device:TPU:35 before, /device:TPU:40 now
where the time goes in v1:
time: 269 us
  waiting for transfers between devices  110 us (41%)
  starting transfers between devices  65.2 us (24%)
  blocking collectives  41.2 us (15%)
  Pallas kernels  35.7 us (13%)
  local copies, waits for them, and re-layouts  9.87 us (4%)
  other arithmetic  5.54 us (2%)
    ppermute x30, waiting for transfers between devices, pull(): return lax.ppermute(value, axis, [(i, (i - step) % N) for i in range(N)])  103 us
    ppermute x30, starting transfers between devices, pull(): return lax.ppermute(value, axis, [(i, (i - step) % N) for i in range(N)])  53.7 us
    all_to_all x1, blocking collectives, spread(): lax.all_to_all(jnp.broadcast_to(value[None], (N, *value.shape)), axis, 0, 0)  28.4 us
    pallas_call x1, Pallas kernels, step(): pl.pallas_call(backward_kernel, in_specs=[SCALAR] + [LOCAL] * 12 + [anywh...  17.7 us
    all_to_all x1, blocking collectives, step(): ups = lax.all_to_all(ups, BAND, 0, 0)  12.8 us
    pallas_call x1, Pallas kernels, step(): pl.pallas_call(forward_kernel, grid_spec=pltpu.PrefetchScalarGridSpec(num...  12.3 us
    all_to_all x1, starting transfers between devices, step(): mixed = lax.all_to_all(dealt, BAND, 0, 0)  5.81 us
    all_to_all x1, starting transfers between devices, step(): first = lax.all_to_all(first.reshape(N, rows, DOWN), 'zh', 0, 0)  5.56 us
  transfers between devices with their start and end apart: 34, of which 20 were waited for; matrix products, arithmetic and copies ran while one was open for 2% of the time, Pallas kernels for 0%

profile of v1, /device:TPU:40, one launch (start us, length us, event | category | flops | bytes accessed | tf_op | source)
XLA Modules:
  0.0 268.6 jit_solution(1510541216932107071)
XLA Ops:
  1.6 3.3 %collective-permute-start.2 = (bf16[32,2304]{1,0:T(8,128)(2,1)S(1)}, bf16[32,2304]{1,0:T(8,128)(2,1)S(1)}, u32[]{:S(2)}, u32[]{:S(2)}) collective-permute-start(bf16[32,2304]{1,0:T(8,128)(2,1)S(1)} %get-tuple-element.24), channel_id=1, source_target_pairs={{0,4},{4,8},{8,12},{12,0},{1,5},{5,9},{9,13},{13,1},{2,6},{6,10},{... | collective-permute-start | bytes 442376 | tf_op jit(solution)/shard_map/ppermute | solution.py:27
  7.1 6.9 %collective-permute-done.2 = bf16[32,2304]{1,0:T(8,128)(2,1)S(1)} collective-permute-done((bf16[32,2304]{1,0:T(8,128)(2,1)S(1)}, bf16[32,2304]{1,0:T(8,128)(2,1)S(1)}, u32[]{:S(2)}, u32[]{:S(2)}) %collective-permute-start.2) | collective-permute-done | bytes 147488 | tf_op jit(solution)/shard_map/ppermute | solution.py:27
  14.2 4.1 %collective-permute-start.1 = (bf16[16,2304]{1,0:T(8,128)(2,1)S(1)}, bf16[16,2304]{1,0:T(8,128)(2,1)S(1)}, u32[]{:S(2)}, u32[]{:S(2)}) collective-permute-start(bf16[16,2304]{1,0:T(8,128)(2,1)S(1)} %slice.152), channel_id=1, source_target_pairs={{0,12},{4,0},{8,4},{12,8},{1,13},{5,1},{9,5},{13,9},{2,14},{6,2},{... | collective-permute-start | bytes 221192 | tf_op jit(solution)/shard_map/ppermute | solution.py:27
  24.4 11.6 %collective-permute-done.5 = bf16[128,2304]{1,0:T(8,128)(2,1)S(1)} collective-permute-done((bf16[128,2304]{1,0:T(8,128)(2,1)S(1)}, bf16[128,2304]{1,0:T(8,128)(2,1)S(1)}, u32[]{:S(2)}, u32[]{:S(2)}) %collective-permute-start.5) | collective-permute-done | bytes 589856 | tf_op jit(solution)/shard_map/ppermute | solution.py:27
  39.7 7.3 %collective-permute-done.8 = bf16[64,2304]{1,0:T(8,128)(2,1)S(1)} collective-permute-done((bf16[64,2304]{1,0:T(8,128)(2,1)S(1)}, bf16[64,2304]{1,0:T(8,128)(2,1)S(1)}, u32[]{:S(2)}, u32[]{:S(2)}) %collective-permute-start.8) | collective-permute-done | bytes 294944 | tf_op jit(solution)/shard_map/ppermute | solution.py:27
  50.0 12.3 %shard_map.67 = (bf16[1024,2304]{1,0:T(8,128)(2,1)}, f32[1024,512]{1,0:T(8,128)}, bf16[1024,512]{1,0:T(8,128)(2,1)}, bf16[4,256,1408]{2,1,0:T(8,128)(2,1)}, bf16[4,4,64,896]{3,2,1,0:T(8,128)(2,1)}) custom-call(s32[2]{0:T(128)} %pad_add_fusion.at_ref, bf16[3,128,2304]{2,1,0:T(8,128)(2,1)} %copy-done, bf16[3,128,2304]{2,1,0:T(8,128)(2,1)} %collective-permute-done.6.near2_ref, ...), custom_call_target="tpu_custom_call" | custom-call | tf_op jit(solution)/shard_map/pallas_call | solution.py:230
  67.4 4.4 %collective-permute-start.16 = (bf16[128,896]{1,0:T(8,128)(2,1)S(1)}, bf16[128,896]{1,0:T(8,128)(2,1)S(1)}, u32[]{:S(2)}, u32[]{:S(2)}) collective-permute-start(bf16[128,896]{1,0:T(8,128)(2,1)S(1)} %bitcast.49), channel_id=1, source_target_pairs={{0,12},{4,0},{8,4},{12,8},{1,13},{5,1},{9,5},{13,9},{2,14},{6,2},{... | collective-permute-start | bytes 688136 | tf_op jit(solution)/shard_map/ppermute | solution.py:27
  71.7 3.9 %collective-permute-done.10 = bf16[128,1408]{1,0:T(8,128)(2,1)S(1)} collective-permute-done((bf16[128,1408]{1,0:T(8,128)(2,1)S(1)}, bf16[128,1408]{1,0:T(8,128)(2,1)S(1)}, u32[]{:S(2)}, u32[]{:S(2)}) %collective-permute-start.10) | collective-permute-done | bytes 360480 | tf_op jit(solution)/shard_map/ppermute | solution.py:27
  75.9 3.1 %collective-permute-start.13 = (bf16[256,1408]{1,0:T(8,128)(2,1)S(1)}, bf16[256,1408]{1,0:T(8,128)(2,1)S(1)}, u32[]{:S(2)}, u32[]{:S(2)}) collective-permute-start(bf16[256,1408]{1,0:T(8,128)(2,1)S(1)} %pad_maximum_fusion.2), channel_id=1, source_target_pairs={{0,3},{1,0},{2,1},{3,2},{4,7},{5,4},{6,5},{7,6},{8,11},{9,8},{10,9... | collective-permute-start | bytes 2162696 | tf_op jit(solution)/shard_map/ppermute | solution.py:27
  79.2 6.5 %collective-permute-done.14 = bf16[128,896]{1,0:T(8,128)(2,1)S(1)} collective-permute-done((bf16[128,896]{1,0:T(8,128)(2,1)S(1)}, bf16[128,896]{1,0:T(8,128)(2,1)S(1)}, u32[]{:S(2)}, u32[]{:S(2)}) %collective-permute-start.14) | collective-permute-done | bytes 229408 | tf_op jit(solution)/shard_map/ppermute | solution.py:27
  87.5 4.1 %collective-permute-start.17 = (bf16[256,896]{1,0:T(8,128)(2,1)}, bf16[256,896]{1,0:T(8,128)(2,1)S(1)}, u32[]{:S(2)}, u32[]{:S(2)}) collective-permute-start(bf16[256,896]{1,0:T(8,128)(2,1)} %pad_maximum_fusion.4), channel_id=1, source_target_pairs={{0,12},{4,0},{8,4},{12,8},{1,13},{5,1},{9,5},{13,9},{2,14},{6,2},{... | collective-permute-start | bytes 1376264 | tf_op jit(solution)/shard_map/ppermute | solution.py:27
  93.7 3.6 %collective-permute-done.11 = bf16[256,1408]{1,0:T(8,128)(2,1)S(1)} collective-permute-done((bf16[256,1408]{1,0:T(8,128)(2,1)S(1)}, bf16[256,1408]{1,0:T(8,128)(2,1)S(1)}, u32[]{:S(2)}, u32[]{:S(2)}) %collective-permute-start.11) | collective-permute-done | bytes 720928 | tf_op jit(solution)/shard_map/ppermute | solution.py:27
  98.4 5.6 %all-to-all-start = ((bf16[4,64,1408]{2,1,0:T(8,128)(2,1)}), bf16[4,64,1408]{2,1,0:T(8,128)(2,1)S(1)}, u32[]{:S(2)}, u32[]{:S(2)}) async-start(bf16[4,64,1408]{2,1,0:T(8,128)(2,1)} %bitcast.15), calls=%async_computation | async-start | bytes 1441792 | tf_op jit(solution)/shard_map/all_to_all | solution.py:263
  104.0 10.5 %collective-permute-done.15 = bf16[256,896]{1,0:T(8,128)(2,1)S(1)} collective-permute-done((bf16[256,896]{1,0:T(8,128)(2,1)}, bf16[256,896]{1,0:T(8,128)(2,1)S(1)}, u32[]{:S(2)}, u32[]{:S(2)}) %collective-permute-start.15) | collective-permute-done | bytes 458784 | tf_op jit(solution)/shard_map/ppermute | solution.py:27
  129.0 5.8 %all-to-all-start.1 = ((bf16[16,8,1152]{2,1,0:T(8,128)(2,1)}), bf16[16,8,1152]{2,1,0:T(8,128)(2,1)S(1)}, u32[]{:S(2)}, u32[]{:S(2)}) async-start(bf16[16,8,1152]{2,1,0:T(8,128)(2,1)} %shard_map.68), calls=%async_computation.1 | async-start | bytes 589824 | tf_op jit(solution)/shard_map/all_to_all | solution.py:274
  136.1 3.9 %all-to-all-done.1.mixed_ref = bf16[16,8,1152]{2,1,0:T(8,128)(2,1)S(1)} async-done(((bf16[16,8,1152]{2,1,0:T(8,128)(2,1)}), bf16[16,8,1152]{2,1,0:T(8,128)(2,1)S(1)}, u32[]{:S(2)}, u32[]{:S(2)}) %all-to-all-start.1) | async-done | bytes 294944 | tf_op jit(solution)/shard_map/all_to_all | solution.py:274
  142.6 12.8 %all_to_all.20.mixed_ref = bf16[16,8,1280]{2,1,0:T(8,128)(2,1)} all-to-all(bf16[16,8,1280]{2,1,0:T(8,128)(2,1)} %shard_map.69), channel_id=1, replica_groups=mesh['y'=4,'zl'=2,'core'=2,'zh'=4,'x'=4] {'y','zl','core'}, dimensions={0} | all-to-all | bytes 655360 | tf_op jit(solution)/shard_map/all_to_all | solution.py:282
  158.1 28.4 %all_to_all.21 = bf16[4,64,1536]{2,1,0:T(8,128)(2,1)S(1)} all-to-all(bf16[4,64,1536]{2,1,0:T(8,128)(2,1)S(1)} %broadcast_in_dim.10), channel_id=1, replica_groups=mesh['y'=4,'zl'=2,'core'=2,'zh'=4,'x'=4] {'zh'}, dimensions={0} | all-to-all | bytes 1572864 | tf_op jit(solution)/shard_map/all_to_all | solution.py:23
  186.5 3.2 %collective-permute-start.21 = (bf16[256,1536]{1,0:T(8,128)(2,1)S(1)}, bf16[256,1536]{1,0:T(8,128)(2,1)S(1)}, u32[]{:S(2)}, u32[]{:S(2)}) collective-permute-start(bf16[256,1536]{1,0:T(8,128)(2,1)S(1)} %bitcast.42), channel_id=1, source_target_pairs={{0,3},{1,0},{2,1},{3,2},{4,7},{5,4},{6,5},{7,6},{8,11},{9,8},{10,9... | collective-permute-start | bytes 2359304 | tf_op jit(solution)/shard_map/ppermute | solution.py:27
  193.0 18.2 %collective-permute-done.25 = bf16[64,896]{1,0:T(8,128)(2,1)S(1)} collective-permute-done((bf16[64,896]{1,0:T(8,128)(2,1)S(1)}, bf16[64,896]{1,0:T(8,128)(2,1)S(1)}, u32[]{:S(2)}, u32[]{:S(2)}) %collective-permute-start.25) | collective-permute-done | bytes 114720 | tf_op jit(solution)/shard_map/ppermute | solution.py:27
  219.6 16.4 %collective-permute-done.30.b4 = bf16[256,896]{1,0:T(8,128)(2,1)S(1)} collective-permute-done((bf16[256,896]{1,0:T(8,128)(2,1)S(1)}, bf16[256,896]{1,0:T(8,128)(2,1)S(1)}, u32[]{:S(2)}, u32[]{:S(2)}) %collective-permute-start.30) | collective-permute-done | bytes 458784 | tf_op jit(solution)/shard_map/ppermute | solution.py:27
  236.2 4.2 %collective-permute-start.29 = (bf16[128,896]{1,0:T(8,128)(2,1)S(1)}, bf16[128,896]{1,0:T(8,128)(2,1)S(1)}, u32[]{:S(2)}, u32[]{:S(2)}) collective-permute-start(bf16[128,896]{1,0:T(8,128)(2,1)S(1)} %slice.162), channel_id=1, source_target_pairs={{0,12},{4,0},{8,4},{12,8},{1,13},{5,1},{9,5},{13,9},{2,14},{6,2},{... | collective-permute-start | bytes 688136 | tf_op jit(solution)/shard_map/ppermute | solution.py:27
  240.4 7.7 %collective-permute-done.31.b3 = bf16[128,896]{1,0:T(8,128)(2,1)S(1)} collective-permute-done((bf16[128,896]{1,0:T(8,128)(2,1)S(1)}, bf16[128,896]{1,0:T(8,128)(2,1)S(1)}, u32[]{:S(2)}, u32[]{:S(2)}) %collective-permute-start.31) | collective-permute-done | bytes 229408 | tf_op jit(solution)/shard_map/ppermute | solution.py:27
  249.7 17.7 %shard_map.71 = (bf16[2304,512]{1,0:T(8,128)(2,1)}, bf16[512,2304]{1,0:T(8,128)(2,1)}, f32[8,128]{1,0:T(8,128)}) custom-call(s32[2]{0:T(128)} %pad_add_fusion.at_ref, bf16[256,1536]{1,0:T(8,128)(2,1)} %bitcast.43, bf16[256,1536]{1,0:T(8,128)(2,1)} %copy-done.7, bf16[128,1536]{1,0:T(8,128)(2,1)} %copy-done.14, bf16[128,1536]{1,0:T(8,128)(2,1)} %copy-done.13, ...), custom_call_target="tpu_custom_call" | custom-call | tf_op jit(solution)/shard_map/pallas_call | solution.py:297
  (130 shorter events, 62.3 us)
Async XLA Ops:
  1.6 12.5 %collective-permute-start.2 = (bf16[32,2304]{1,0:T(8,128)(2,1)S(1)}, bf16[32,2304]{1,0:T(8,128)(2,1)S(1)}, u32[]{:S(2)}, u32[]{:S(2)}) collective-permute-start(bf16[32,2304]{1,0:T(8,128)(2,1)S(1)} %get-tuple-element.24), channel_id=1, source_target_pairs={{0,4},{4,8},{8,12},{12,0},{1,5},{5,9},{9,13},{13,1},{2,6},{6,10},{... | collective-permute-start | bytes 442376 | tf_op jit(solution)/shard_map/ppermute | solution.py:27
  21.1 14.9 %collective-permute-start.5 = (bf16[128,2304]{1,0:T(8,128)(2,1)S(1)}, bf16[128,2304]{1,0:T(8,128)(2,1)S(1)}, u32[]{:S(2)}, u32[]{:S(2)}) collective-permute-start(bf16[128,2304]{1,0:T(8,128)(2,1)S(1)} %constant_dynamic-update-slice_fusion), channel_id=1, source_target_pairs={{0,1},{1,2},{2,3},{3,0},{4,5},{5,6},{6,7},{7,4},{8,9},{9,10},{10,1... | collective-permute-start | bytes 1769480 | tf_op jit(solution)/shard_map/ppermute | solution.py:27
  22.6 13.3 %collective-permute-start.4 = (bf16[128,2304]{1,0:T(8,128)(2,1)S(1)}, bf16[128,2304]{1,0:T(8,128)(2,1)S(1)}, u32[]{:S(2)}, u32[]{:S(2)}) collective-permute-start(bf16[128,2304]{1,0:T(8,128)(2,1)S(1)} %constant_dynamic-update-slice_fusion), channel_id=1, source_target_pairs={{0,3},{1,0},{2,1},{3,2},{4,7},{5,4},{6,5},{7,6},{8,11},{9,8},{10,9... | collective-permute-start | bytes 1769480 | tf_op jit(solution)/shard_map/ppermute | solution.py:27
  36.2 13.1 %collective-permute-start.6 = (bf16[3,128,2304]{2,1,0:T(8,128)(2,1)S(1)}, bf16[3,128,2304]{2,1,0:T(8,128)(2,1)}, u32[]{:S(2)}, u32[]{:S(2)}) collective-permute-start(bf16[3,128,2304]{2,1,0:T(8,128)(2,1)S(1)} %pad_maximum_fusion.near_ref), channel_id=1, source_target_pairs={{0,16},{16,0},{1,17},{17,1},{2,18},{18,2},{3,19},{19,3},{4,20},{20... | collective-permute-start | bytes 5308424 | tf_op jit(solution)/shard_map/ppermute | solution.py:224
  63.9 11.8 %collective-permute-start.10 = (bf16[128,1408]{1,0:T(8,128)(2,1)S(1)}, bf16[128,1408]{1,0:T(8,128)(2,1)S(1)}, u32[]{:S(2)}, u32[]{:S(2)}) collective-permute-start(bf16[128,1408]{1,0:T(8,128)(2,1)S(1)} %get-tuple-element.27), channel_id=1, source_target_pairs={{0,1},{1,2},{2,3},{3,0},{4,5},{5,6},{6,7},{7,4},{8,9},{9,10},{10,1... | collective-permute-start | bytes 1081352 | tf_op jit(solution)/shard_map/ppermute | solution.py:27
  67.4 19.2 %collective-permute-start.16 = (bf16[128,896]{1,0:T(8,128)(2,1)S(1)}, bf16[128,896]{1,0:T(8,128)(2,1)S(1)}, u32[]{:S(2)}, u32[]{:S(2)}) collective-permute-start(bf16[128,896]{1,0:T(8,128)(2,1)S(1)} %bitcast.49), channel_id=1, source_target_pairs={{0,12},{4,0},{8,4},{12,8},{1,13},{5,1},{9,5},{13,9},{2,14},{6,2},{... | collective-permute-start | bytes 688136 | tf_op jit(solution)/shard_map/ppermute | solution.py:27
  71.7 13.9 %collective-permute-start.14 = (bf16[128,896]{1,0:T(8,128)(2,1)S(1)}, bf16[128,896]{1,0:T(8,128)(2,1)S(1)}, u32[]{:S(2)}, u32[]{:S(2)}) collective-permute-start(bf16[128,896]{1,0:T(8,128)(2,1)S(1)} %bitcast.50), channel_id=1, source_target_pairs={{0,4},{4,8},{8,12},{12,0},{1,5},{5,9},{9,13},{13,1},{2,6},{6,10},{... | collective-permute-start | bytes 688136 | tf_op jit(solution)/shard_map/ppermute | solution.py:27
  75.9 17.8 %collective-permute-start.13 = (bf16[256,1408]{1,0:T(8,128)(2,1)S(1)}, bf16[256,1408]{1,0:T(8,128)(2,1)S(1)}, u32[]{:S(2)}, u32[]{:S(2)}) collective-permute-start(bf16[256,1408]{1,0:T(8,128)(2,1)S(1)} %pad_maximum_fusion.2), channel_id=1, source_target_pairs={{0,3},{1,0},{2,1},{3,2},{4,7},{5,4},{6,5},{7,6},{8,11},{9,8},{10,9... | collective-permute-start | bytes 2162696 | tf_op jit(solution)/shard_map/ppermute | solution.py:27
  79.1 18.2 %collective-permute-start.11 = (bf16[256,1408]{1,0:T(8,128)(2,1)S(1)}, bf16[256,1408]{1,0:T(8,128)(2,1)S(1)}, u32[]{:S(2)}, u32[]{:S(2)}) collective-permute-start(bf16[256,1408]{1,0:T(8,128)(2,1)S(1)} %pad_maximum_fusion.1), channel_id=1, source_target_pairs={{0,1},{1,2},{2,3},{3,0},{4,5},{5,6},{6,7},{7,4},{8,9},{9,10},{10,1... | collective-permute-start | bytes 2162696 | tf_op jit(solution)/shard_map/ppermute | solution.py:27
  86.6 27.9 %collective-permute-start.15 = (bf16[256,896]{1,0:T(8,128)(2,1)}, bf16[256,896]{1,0:T(8,128)(2,1)S(1)}, u32[]{:S(2)}, u32[]{:S(2)}) collective-permute-start(bf16[256,896]{1,0:T(8,128)(2,1)} %pad_maximum_fusion.3), channel_id=1, source_target_pairs={{0,4},{4,8},{8,12},{12,0},{1,5},{5,9},{9,13},{13,1},{2,6},{6,10},{... | collective-permute-start | bytes 1376264 | tf_op jit(solution)/shard_map/ppermute | solution.py:27
  87.5 27.0 %collective-permute-start.17 = (bf16[256,896]{1,0:T(8,128)(2,1)}, bf16[256,896]{1,0:T(8,128)(2,1)S(1)}, u32[]{:S(2)}, u32[]{:S(2)}) collective-permute-start(bf16[256,896]{1,0:T(8,128)(2,1)} %pad_maximum_fusion.4), channel_id=1, source_target_pairs={{0,12},{4,0},{8,4},{12,8},{1,13},{5,1},{9,5},{13,9},{2,14},{6,2},{... | collective-permute-start | bytes 1376264 | tf_op jit(solution)/shard_map/ppermute | solution.py:27
  98.4 27.6 %all-to-all-start = ((bf16[4,64,1408]{2,1,0:T(8,128)(2,1)}), bf16[4,64,1408]{2,1,0:T(8,128)(2,1)S(1)}, u32[]{:S(2)}, u32[]{:S(2)}) async-start(bf16[4,64,1408]{2,1,0:T(8,128)(2,1)} %bitcast.15), calls=%async_computation | async-start | bytes 1441792 | tf_op jit(solution)/shard_map/all_to_all | solution.py:263
  129.0 11.0 %all-to-all-start.1 = ((bf16[16,8,1152]{2,1,0:T(8,128)(2,1)}), bf16[16,8,1152]{2,1,0:T(8,128)(2,1)S(1)}, u32[]{:S(2)}, u32[]{:S(2)}) async-start(bf16[16,8,1152]{2,1,0:T(8,128)(2,1)} %shard_map.68), calls=%async_computation.1 | async-start | bytes 589824 | tf_op jit(solution)/shard_map/all_to_all | solution.py:274
  186.5 29.7 %collective-permute-start.23 = (bf16[256,1536]{1,0:T(8,128)(2,1)S(1)}, bf16[256,1536]{1,0:T(8,128)(2,1)S(1)}, u32[]{:S(2)}, u32[]{:S(2)}) collective-permute-start(bf16[256,1536]{1,0:T(8,128)(2,1)S(1)} %bitcast.41), channel_id=1, source_target_pairs={{0,1},{1,2},{2,3},{3,0},{4,5},{5,6},{6,7},{7,4},{8,9},{9,10},{10,1... | collective-permute-start | bytes 2359304 | tf_op jit(solution)/shard_map/ppermute | solution.py:27
  186.5 30.0 %collective-permute-start.21 = (bf16[256,1536]{1,0:T(8,128)(2,1)S(1)}, bf16[256,1536]{1,0:T(8,128)(2,1)S(1)}, u32[]{:S(2)}, u32[]{:S(2)}) collective-permute-start(bf16[256,1536]{1,0:T(8,128)(2,1)S(1)} %bitcast.42), channel_id=1, source_target_pairs={{0,3},{1,0},{2,1},{3,2},{4,7},{5,4},{6,5},{7,6},{8,11},{9,8},{10,9... | collective-permute-start | bytes 2359304 | tf_op jit(solution)/shard_map/ppermute | solution.py:27
  189.8 22.2 %collective-permute-start.27 = (bf16[64,896]{1,0:T(8,128)(2,1)S(1)}, bf16[64,896]{1,0:T(8,128)(2,1)S(1)}, u32[]{:S(2)}, u32[]{:S(2)}) collective-permute-start(bf16[64,896]{1,0:T(8,128)(2,1)S(1)} %copy-done.17), channel_id=1, source_target_pairs={{0,1},{1,2},{2,3},{3,0},{4,5},{5,6},{6,7},{7,4},{8,9},{9,10},{10,1... | collective-permute-start | bytes 344072 | tf_op jit(solution)/shard_map/ppermute | solution.py:27
  189.8 22.1 %collective-permute-start.26 = (bf16[64,896]{1,0:T(8,128)(2,1)S(1)}, bf16[64,896]{1,0:T(8,128)(2,1)S(1)}, u32[]{:S(2)}, u32[]{:S(2)}) collective-permute-start(bf16[64,896]{1,0:T(8,128)(2,1)S(1)} %copy-done.17), channel_id=1, source_target_pairs={{0,2},{1,3},{2,0},{3,1},{4,6},{5,7},{6,4},{7,5},{8,10},{9,11},{10,... | collective-permute-start | bytes 344072 | tf_op jit(solution)/shard_map/ppermute | solution.py:27
  191.7 19.5 %collective-permute-start.25 = (bf16[64,896]{1,0:T(8,128)(2,1)S(1)}, bf16[64,896]{1,0:T(8,128)(2,1)S(1)}, u32[]{:S(2)}, u32[]{:S(2)}) collective-permute-start(bf16[64,896]{1,0:T(8,128)(2,1)S(1)} %copy-done.17), channel_id=1, source_target_pairs={{0,3},{1,0},{2,1},{3,2},{4,7},{5,4},{6,5},{7,6},{8,11},{9,8},{10,9... | collective-permute-start | bytes 344072 | tf_op jit(solution)/shard_map/ppermute | solution.py:27
  212.0 24.1 %collective-permute-start.30 = (bf16[256,896]{1,0:T(8,128)(2,1)S(1)}, bf16[256,896]{1,0:T(8,128)(2,1)S(1)}, u32[]{:S(2)}, u32[]{:S(2)}) collective-permute-start(bf16[256,896]{1,0:T(8,128)(2,1)S(1)} %constant_dynamic-update-slice_fusion.5.b0), channel_id=1, source_target_pairs={{0,4},{4,8},{8,12},{12,0},{1,5},{5,9},{9,13},{13,1},{2,6},{6,10},{... | collective-permute-start | bytes 1376264 | tf_op jit(solution)/shard_map/ppermute | solution.py:27
  213.1 23.1 %collective-permute-start.28 = (bf16[256,896]{1,0:T(8,128)(2,1)S(1)}, bf16[256,896]{1,0:T(8,128)(2,1)S(1)}, u32[]{:S(2)}, u32[]{:S(2)}) collective-permute-start(bf16[256,896]{1,0:T(8,128)(2,1)S(1)} %constant_dynamic-update-slice_fusion.5.b0), channel_id=1, source_target_pairs={{0,12},{4,0},{8,4},{12,8},{1,13},{5,1},{9,5},{13,9},{2,14},{6,2},{... | collective-permute-start | bytes 1376264 | tf_op jit(solution)/shard_map/ppermute | solution.py:27
  216.2 31.9 %collective-permute-start.24 = (bf16[128,1536]{1,0:T(8,128)(2,1)S(1)}, bf16[128,1536]{1,0:T(8,128)(2,1)S(1)}, u32[]{:S(2)}, u32[]{:S(2)}) collective-permute-start(bf16[128,1536]{1,0:T(8,128)(2,1)S(1)} %slice.161), channel_id=1, source_target_pairs={{0,1},{1,2},{2,3},{3,0},{4,5},{5,6},{6,7},{7,4},{8,9},{9,10},{10,1... | collective-permute-start | bytes 1179656 | tf_op jit(solution)/shard_map/ppermute | solution.py:27
  216.5 31.6 %collective-permute-start.22 = (bf16[128,1536]{1,0:T(8,128)(2,1)S(1)}, bf16[128,1536]{1,0:T(8,128)(2,1)S(1)}, u32[]{:S(2)}, u32[]{:S(2)}) collective-permute-start(bf16[128,1536]{1,0:T(8,128)(2,1)S(1)} %slice.160), channel_id=1, source_target_pairs={{0,3},{1,0},{2,1},{3,2},{4,7},{5,4},{6,5},{7,6},{8,11},{9,8},{10,9... | collective-permute-start | bytes 1179656 | tf_op jit(solution)/shard_map/ppermute | solution.py:27
  236.1 12.0 %collective-permute-start.31 = (bf16[128,896]{1,0:T(8,128)(2,1)S(1)}, bf16[128,896]{1,0:T(8,128)(2,1)S(1)}, u32[]{:S(2)}, u32[]{:S(2)}) collective-permute-start(bf16[128,896]{1,0:T(8,128)(2,1)S(1)} %slice.163), channel_id=1, source_target_pairs={{0,4},{4,8},{8,12},{12,0},{1,5},{5,9},{9,13},{13,1},{2,6},{6,10},{... | collective-permute-start | bytes 688136 | tf_op jit(solution)/shard_map/ppermute | solution.py:27
  236.2 11.9 %collective-permute-start.29 = (bf16[128,896]{1,0:T(8,128)(2,1)S(1)}, bf16[128,896]{1,0:T(8,128)(2,1)S(1)}, u32[]{:S(2)}, u32[]{:S(2)}) collective-permute-start(bf16[128,896]{1,0:T(8,128)(2,1)S(1)} %slice.162), channel_id=1, source_target_pairs={{0,12},{4,0},{8,4},{12,8},{1,13},{5,1},{9,5},{13,9},{2,14},{6,2},{... | collective-permute-start | bytes 688136 | tf_op jit(solution)/shard_map/ppermute | solution.py:27
  (31 other events, 338.1 us)

commit v2 on v1

--- a/solution.py
+++ b/solution.py
@@ -14,13 +14,9 @@
 N = 4
 BANDS = 16
 LANES = 128
-DOWN = 1408
+DOWN = 1536
 UP = 1536
 Shape = jax.ShapeDtypeStruct
-
-
-def spread(value, axis):
-    return lax.all_to_all(jnp.broadcast_to(value[None], (N, *value.shape)), axis, 0, 0)
 
 
 def pull(value, axis, step):
@@ -79,57 +75,73 @@
 
 
 def backward_kernel(
-    at_ref, a0, a1, a2, a3, a4, b0, b1, b2, b3, b4, dec_ref, linear_ref, active_any, gathered_any,
-    enc_out, dec_out, found_ref, up_ref, grad_ref, active_ref, gathered_ref, sems,
+    a0, a1, a2, a3, a4, b0, b1, b2, b3, b4, dec_any, linear_any, active_any, gathered_any,
+    enc_out, dec_out, found_ref, up_ref, extra_ref, grad_ref, dec_ref, linear_ref, active_ref, gathered_ref, sems, up_sems,
 ):
     block = a0.shape[0]
     rows = block // N
     width = up_ref.shape[1]
     rest = width - UP
-    copies = [
-        pltpu.make_async_copy(active_any, active_ref, sems.at[0]),
-        pltpu.make_async_copy(gathered_any, gathered_ref, sems.at[1]),
-    ]
-    for copy in copies:
+
+    def fetch(source, target, sem):
+        copy = pltpu.make_async_copy(source, target, sem)
         copy.start()
-    for x, pieces in enumerate(((a0,), (a1,), (a2, a3), (a4,))):
-        z = 0
-        for piece in pieces:
-            for i in range(piece.shape[0] // rows):
-                place = block * x + rows * ((z + N - at_ref[1]) % N)
-                up_ref[pl.ds(pl.multiple_of(place, rows), rows), :UP] = piece[rows * i : rows * i + rows]
-                z += 1
-    found = jnp.zeros((8, LANES), F32)
-    for z, pieces in enumerate(((b0,), (b1,), (b2, b3), (b4,))):
-        x = 0
-        for piece in pieces:
-            for i in range(piece.shape[0] // rows):
-                place = block * x + rows * z
-                up_ref[place : place + rows, UP:] = piece[rows * i : rows * i + rows, :rest]
-                found = found + piece[rows * i : rows * i + 8, rest:].astype(F32)
-                x += 1
-    found_ref[...] = found
+        return copy
+
+    whole = [fetch(dec_any, dec_ref, sems.at[0])]
+    parts = []
+    for x in range(N):
+        here, at = [], block * x
+        for piece in ((a0,), (a1,), (a2, a3), (a4,))[x]:
+            size = piece.shape[0]
+            here.append(fetch(piece, up_ref.at[at : at + size, :UP], up_sems.at[x, len(here)]))
+            at += size
+        for z in range(N):
+            piece, i = ((b0, x), (b1, x), (b2, x) if x < 2 else (b3, x - 2), (b4, x))[z]
+            at = block * x + rows * z
+            source = piece.at[rows * i : rows * i + rows]
+            here.append(fetch(source.at[:, :rest], up_ref.at[at : at + rows, UP:], up_sems.at[x, len(here)]))
+            here.append(fetch(source.at[:, rest:], extra_ref.at[at : at + rows], up_sems.at[x, len(here)]))
+        parts.append(here)
+        if x == 0:
+            whole.append(fetch(linear_any, linear_ref, sems.at[1]))
+    whole.append(fetch(active_any, active_ref, sems.at[2]))
+    whole.append(fetch(gathered_any, gathered_ref, sems.at[3]))
+    whole[0].wait()
+    whole[1].wait()
 
     def first(x, _):
+        for k in range(N):
+
+            @pl.when(x == k)
+            def _():
+                for copy in parts[k]:
+                    copy.wait()
+
         span = pl.ds(pl.multiple_of(block * x, block), block)
         grads = lax.dot_general(up_ref[span], dec_ref[...], (((1,), (1,)), ((), ())), preferred_element_type=F32)
         grad_ref[span] = (2.0 * linear_ref[span] * grads).astype(BF)
         return 0
 
     lax.fori_loop(0, N, first, 0)
+    found = jnp.zeros((8, LANES), F32)
+    for i in range(N * N):
+        found = found + extra_ref[rows * i : rows * i + 8].astype(F32)
+    found_ref[...] = jnp.sum(found, axis=0, keepdims=True)
+
     contract = (((0,), (0,)), ((), ()))
-    copies[0].wait()
     step = 2 * LANES
+    whole[2].wait()
 
     def second(i, _):
         span = pl.ds(pl.multiple_of(step * i, step), step)
-        dec_out[:, span] = lax.dot_general(
-            active_ref[...], up_ref[:, span], contract, preferred_element_type=F32
+        dec_out[span] = lax.dot_general(
+            active_ref[:, span], up_ref[...], contract, preferred_element_type=F32
         ).astype(BF)
         return 0
 
-    lax.fori_loop(0, width // step, second, 0)
-    copies[1].wait()
+    lax.fori_loop(0, active_ref.shape[1] // step, second, 0)
+    whole[3].wait()
 
     def third(i, _):
         span = pl.ds(pl.multiple_of(step * i, step), step)
@@ -287,27 +299,31 @@
         out_specs=[LOCAL, LOCAL],
     )(which, ups)
 
+    up_a = jnp.concatenate(gather_ring(up_a, "zh"), 0)
     others = [pull(up_b, "x", o) for o in range(1, N)]
     up_b = jnp.concatenate([up_b] + others, 0)
-    up_a = spread(up_a, "zh")
-    up_a = gather_ring(up_a.reshape(block, UP), "x")
+    up_a = gather_ring(up_a, "x")
     up_b = gather_ring(up_b, "zh")
 
     anywhere = pl.BlockSpec(memory_space=pl.ANY)
     enc_grads, dec_grads, found = pl.pallas_call(
         backward_kernel,
-        in_specs=[SCALAR] + [LOCAL] * 12 + [anywhere] * 2,
+        in_specs=[anywhere] * 14,
         out_specs=[LOCAL] * 3,
-        out_shape=[Shape((width, latents), BF), Shape((latents, width), BF), Shape((8, LANES), F32)],
+        out_shape=[Shape((width, latents), BF), Shape((latents, width), BF), Shape((1, LANES), F32)],
         scratch_shapes=[
             pltpu.VMEM((total, width), BF),
+            pltpu.VMEM((total, LANES), BF),
             pltpu.VMEM((total, latents), BF),
+            pltpu.VMEM((latents, width), BF),
+            pltpu.VMEM((total, latents), F32),
             pltpu.VMEM((total, latents), BF),
             pltpu.VMEM((total, width), BF),
-            pltpu.SemaphoreType.DMA((2,)),
+            pltpu.SemaphoreType.DMA((4,)),
+            pltpu.SemaphoreType.DMA((N, 2 + 2 * N)),
         ],
-    )(at, *up_a, *up_b, decoder, linear, active, gathered)
-    losses = jnp.sum(found, axis=0)[:BANDS] / divisor
+    )(*up_a, *up_b, decoder, linear, active, gathered)
+    losses = found[0, :BANDS] / divisor
     return losses, enc_grads, dec_grads
 
 

time: 269 us -> 286 us (1.063)
  the two profiles are of different devices: /device:TPU:40 before, /device:TPU:8 now
where the time goes in v2:
time: 286 us
  waiting for transfers between devices  148 us (52%)
  starting transfers between devices  74.3 us (26%)
  Pallas kernels  34.4 us (12%)
  blocking collectives  12.9 us (5%)
  local copies, waits for them, and re-layouts  10.7 us (4%)
  other arithmetic  4.71 us (2%)
    ppermute x34, waiting for transfers between devices, pull(): return lax.ppermute(value, axis, [(i, (i - step) % N) for i in range(N)])  142 us
    ppermute x34, starting transfers between devices, pull(): return lax.ppermute(value, axis, [(i, (i - step) % N) for i in range(N)])  64.1 us
    pallas_call x1, Pallas kernels, step(): pl.pallas_call(backward_kernel, in_specs=[anywhere] * 14, out_specs=[LOCA...  16.4 us
    all_to_all x1, blocking collectives, step(): ups = lax.all_to_all(ups, BAND, 0, 0)  12.9 us
    pallas_call x1, Pallas kernels, step(): pl.pallas_call(forward_kernel, grid_spec=pltpu.PrefetchScalarGridSpec(num...  12.2 us
    unnamed x53, local copies, waits for them, and re-layouts  6.08 us
  transfers between devices with their start and end apart: 38, of which 23 were waited for; matrix products, arithmetic and copies ran while one was open for 3% of the time, Pallas kernels for 0%

profile of v2, /device:TPU:8, one launch (start us, length us, event | category | flops | bytes accessed | tf_op | source)
XLA Modules:
  0.0 285.7 jit_solution(6544808179731309179)
XLA Ops:
  1.6 3.3 %collective-permute-start.2 = (bf16[32,2304]{1,0:T(8,128)(2,1)S(1)}, bf16[32,2304]{1,0:T(8,128)(2,1)S(1)}, u32[]{:S(2)}, u32[]{:S(2)}) collective-permute-start(bf16[32,2304]{1,0:T(8,128)(2,1)S(1)} %get-tuple-element.24), channel_id=1, source_target_pairs={{0,4},{4,8},{8,12},{12,0},{1,5},{5,9},{9,13},{13,1},{2,6},{6,10},{... | collective-permute-start | bytes 442376 | tf_op jit(solution)/shard_map/ppermute | solution.py:23
  8.0 4.3 %collective-permute-done.2 = bf16[32,2304]{1,0:T(8,128)(2,1)S(1)} collective-permute-done((bf16[32,2304]{1,0:T(8,128)(2,1)S(1)}, bf16[32,2304]{1,0:T(8,128)(2,1)S(1)}, u32[]{:S(2)}, u32[]{:S(2)}) %collective-permute-start.2) | collective-permute-done | bytes 147488 | tf_op jit(solution)/shard_map/ppermute | solution.py:23
  18.9 4.3 %collective-permute-done.1 = bf16[16,2304]{1,0:T(8,128)(2,1)S(1)} collective-permute-done((bf16[16,2304]{1,0:T(8,128)(2,1)S(1)}, bf16[16,2304]{1,0:T(8,128)(2,1)S(1)}, u32[]{:S(2)}, u32[]{:S(2)}) %collective-permute-start.1) | collective-permute-done | bytes 73760 | tf_op jit(solution)/shard_map/ppermute | solution.py:23
  26.6 11.1 %collective-permute-done.5 = bf16[128,2304]{1,0:T(8,128)(2,1)S(1)} collective-permute-done((bf16[128,2304]{1,0:T(8,128)(2,1)S(1)}, bf16[128,2304]{1,0:T(8,128)(2,1)S(1)}, u32[]{:S(2)}, u32[]{:S(2)}) %collective-permute-start.5) | collective-permute-done | bytes 589856 | tf_op jit(solution)/shard_map/ppermute | solution.py:23
  41.4 7.3 %collective-permute-done.8 = bf16[64,2304]{1,0:T(8,128)(2,1)S(1)} collective-permute-done((bf16[64,2304]{1,0:T(8,128)(2,1)S(1)}, bf16[64,2304]{1,0:T(8,128)(2,1)S(1)}, u32[]{:S(2)}, u32[]{:S(2)}) %collective-permute-start.8) | collective-permute-done | bytes 294944 | tf_op jit(solution)/shard_map/ppermute | solution.py:23
  51.8 12.2 %shard_map.67 = (bf16[1024,2304]{1,0:T(8,128)(2,1)}, f32[1024,512]{1,0:T(8,128)}, bf16[1024,512]{1,0:T(8,128)(2,1)}, bf16[4,256,1536]{2,1,0:T(8,128)(2,1)}, bf16[4,4,64,768]{3,2,1,0:T(8,128)(2,1)}) custom-call(s32[2]{0:T(128)} %pad_add_fusion.at_ref, bf16[3,128,2304]{2,1,0:T(8,128)(2,1)} %copy-done, bf16[3,128,2304]{2,1,0:T(8,128)(2,1)} %collective-permute-done.6.near2_ref, ...), custom_call_target="tpu_custom_call" | custom-call | tf_op jit(solution)/shard_map/pallas_call | solution.py:242
  69.0 9.2 %collective-permute-done.10 = bf16[128,1536]{1,0:T(8,128)(2,1)S(1)} collective-permute-done((bf16[128,1536]{1,0:T(8,128)(2,1)S(1)}, bf16[128,1536]{1,0:T(8,128)(2,1)S(1)}, u32[]{:S(2)}, u32[]{:S(2)}) %collective-permute-start.10) | collective-permute-done | bytes 393248 | tf_op jit(solution)/shard_map/ppermute | solution.py:23
  82.6 3.7 %collective-permute-start.14 = (bf16[128,768]{1,0:T(8,128)(2,1)S(1)}, bf16[128,768]{1,0:T(8,128)(2,1)S(1)}, u32[]{:S(2)}, u32[]{:S(2)}) collective-permute-start(bf16[128,768]{1,0:T(8,128)(2,1)S(1)} %bitcast.47), channel_id=1, source_target_pairs={{0,4},{4,8},{8,12},{12,0},{1,5},{5,9},{9,13},{13,1},{2,6},{6,10},{... | collective-permute-start | bytes 589832 | tf_op jit(solution)/shard_map/ppermute | solution.py:23
  86.8 8.6 %collective-permute-done.14 = bf16[128,768]{1,0:T(8,128)(2,1)S(1)} collective-permute-done((bf16[128,768]{1,0:T(8,128)(2,1)S(1)}, bf16[128,768]{1,0:T(8,128)(2,1)S(1)}, u32[]{:S(2)}, u32[]{:S(2)}) %collective-permute-start.14) | collective-permute-done | bytes 196640 | tf_op jit(solution)/shard_map/ppermute | solution.py:23
  97.6 3.7 %collective-permute-done.11 = bf16[256,1536]{1,0:T(8,128)(2,1)S(1)} collective-permute-done((bf16[256,1536]{1,0:T(8,128)(2,1)S(1)}, bf16[256,1536]{1,0:T(8,128)(2,1)S(1)}, u32[]{:S(2)}, u32[]{:S(2)}) %collective-permute-start.11) | collective-permute-done | bytes 786464 | tf_op jit(solution)/shard_map/ppermute | solution.py:23
  102.5 5.0 %all-to-all-start = ((bf16[4,64,1536]{2,1,0:T(8,128)(2,1)}), bf16[4,64,1536]{2,1,0:T(8,128)(2,1)S(1)}, u32[]{:S(2)}, u32[]{:S(2)}) async-start(bf16[4,64,1536]{2,1,0:T(8,128)(2,1)} %bitcast.15), calls=%async_computation | async-start | bytes 1572864 | tf_op jit(solution)/shard_map/all_to_all | solution.py:275
  108.5 4.2 %collective-permute-start.17 = (bf16[256,768]{1,0:T(8,128)(2,1)S(1)}, bf16[256,768]{1,0:T(8,128)(2,1)S(1)}, u32[]{:S(2)}, u32[]{:S(2)}) collective-permute-start(bf16[256,768]{1,0:T(8,128)(2,1)S(1)} %pad_maximum_fusion.4), channel_id=1, source_target_pairs={{0,12},{4,0},{8,4},{12,8},{1,13},{5,1},{9,5},{13,9},{2,14},{6,2},{... | collective-permute-start | bytes 1179656 | tf_op jit(solution)/shard_map/ppermute | solution.py:23
  112.9 29.7 %collective-permute-done.17 = bf16[256,768]{1,0:T(8,128)(2,1)S(1)} collective-permute-done((bf16[256,768]{1,0:T(8,128)(2,1)S(1)}, bf16[256,768]{1,0:T(8,128)(2,1)S(1)}, u32[]{:S(2)}, u32[]{:S(2)}) %collective-permute-start.17) | collective-permute-done | bytes 393248 | tf_op jit(solution)/shard_map/ppermute | solution.py:23
  145.5 3.4 %collective-permute-done.20.b3 = bf16[64,768]{1,0:T(8,128)(2,1)S(1)} collective-permute-done((bf16[64,768]{1,0:T(8,128)(2,1)S(1)}, bf16[64,768]{1,0:T(8,128)(2,1)S(1)}, u32[]{:S(2)}, u32[]{:S(2)}) %collective-permute-start.20) | collective-permute-done | bytes 98336 | tf_op jit(solution)/shard_map/ppermute | solution.py:23
  154.6 5.0 %all-to-all-start.1 = ((bf16[16,8,1152]{2,1,0:T(8,128)(2,1)}), bf16[16,8,1152]{2,1,0:T(8,128)(2,1)S(1)}, u32[]{:S(2)}, u32[]{:S(2)}) async-start(bf16[16,8,1152]{2,1,0:T(8,128)(2,1)} %shard_map.68), calls=%async_computation.1 | async-start | bytes 589824 | tf_op jit(solution)/shard_map/all_to_all | solution.py:286
  160.9 4.5 %all-to-all-done.1.mixed_ref = bf16[16,8,1152]{2,1,0:T(8,128)(2,1)S(1)} async-done(((bf16[16,8,1152]{2,1,0:T(8,128)(2,1)}), bf16[16,8,1152]{2,1,0:T(8,128)(2,1)S(1)}, u32[]{:S(2)}, u32[]{:S(2)}) %all-to-all-start.1) | async-done | bytes 294944 | tf_op jit(solution)/shard_map/all_to_all | solution.py:286
  168.0 12.9 %all_to_all.15.mixed_ref = bf16[16,8,1280]{2,1,0:T(8,128)(2,1)} all-to-all(bf16[16,8,1280]{2,1,0:T(8,128)(2,1)} %shard_map.69), channel_id=1, replica_groups=mesh['y'=4,'zl'=2,'core'=2,'zh'=4,'x'=4] {'y','zl','core'}, dimensions={0} | all-to-all | bytes 655360 | tf_op jit(solution)/shard_map/all_to_all | solution.py:294
  187.7 8.5 %collective-permute-done.23 = bf16[64,1536]{1,0:T(8,128)(2,1)S(1)} collective-permute-done((bf16[64,1536]{1,0:T(8,128)(2,1)}, bf16[64,1536]{1,0:T(8,128)(2,1)S(1)}, u32[]{:S(2)}, u32[]{:S(2)}) %collective-permute-start.23) | collective-permute-done | bytes 196640 | tf_op jit(solution)/shard_map/ppermute | solution.py:23
  200.5 4.6 %collective-permute-done.22 = bf16[32,1536]{1,0:T(8,128)(2,1)S(1)} collective-permute-done((bf16[32,1536]{1,0:T(8,128)(2,1)S(1)}, bf16[32,1536]{1,0:T(8,128)(2,1)S(1)}, u32[]{:S(2)}, u32[]{:S(2)}) %collective-permute-start.22) | collective-permute-done | bytes 98336 | tf_op jit(solution)/shard_map/ppermute | solution.py:23
  211.7 18.0 %collective-permute-done.29 = bf16[64,896]{1,0:T(8,128)(2,1)S(1)} collective-permute-done((bf16[64,896]{1,0:T(8,128)(2,1)S(1)}, bf16[64,896]{1,0:T(8,128)(2,1)S(1)}, u32[]{:S(2)}, u32[]{:S(2)}) %collective-permute-start.29) | collective-permute-done | bytes 114720 | tf_op jit(solution)/shard_map/ppermute | solution.py:23
  238.2 15.6 %collective-permute-done.34.b4 = bf16[256,896]{1,0:T(8,128)(2,1)S(1)} collective-permute-done((bf16[256,896]{1,0:T(8,128)(2,1)S(1)}, bf16[256,896]{1,0:T(8,128)(2,1)S(1)}, u32[]{:S(2)}, u32[]{:S(2)}) %collective-permute-start.34) | collective-permute-done | bytes 458784 | tf_op jit(solution)/shard_map/ppermute | solution.py:23
  254.0 4.2 %collective-permute-start.33 = (bf16[128,896]{1,0:T(8,128)(2,1)S(1)}, bf16[128,896]{1,0:T(8,128)(2,1)S(1)}, u32[]{:S(2)}, u32[]{:S(2)}) collective-permute-start(bf16[128,896]{1,0:T(8,128)(2,1)S(1)} %slice.172), channel_id=1, source_target_pairs={{0,12},{4,0},{8,4},{12,8},{1,13},{5,1},{9,5},{13,9},{2,14},{6,2},{... | collective-permute-start | bytes 688136 | tf_op jit(solution)/shard_map/ppermute | solution.py:23
  258.2 8.3 %collective-permute-done.35.b3 = bf16[128,896]{1,0:T(8,128)(2,1)S(1)} collective-permute-done((bf16[128,896]{1,0:T(8,128)(2,1)S(1)}, bf16[128,896]{1,0:T(8,128)(2,1)S(1)}, u32[]{:S(2)}, u32[]{:S(2)}) %collective-permute-start.35) | collective-permute-done | bytes 229408 | tf_op jit(solution)/shard_map/ppermute | solution.py:23
  268.2 16.4 %shard_map.71 = (bf16[2304,512]{1,0:T(8,128)(2,1)}, bf16[512,2304]{1,0:T(8,128)(2,1)}, f32[1,128]{1,0:T(1,128)}) custom-call(bf16[256,1536]{1,0:T(8,128)(2,1)} %copy-done.7, bf16[256,1536]{1,0:T(8,128)(2,1)} %copy-done.5, bf16[128,1536]{1,0:T(8,128)(2,1)} %copy-done.14, bf16[128,1536]{1,0:T(8,128)(2,1)} %copy-done.13, bf16[256,1536]{1,0:T(8,128)(2,1)} %copy-done.4, ...), custom_call_target="tpu_custom_call" | custom-call | tf_op jit(solution)/shard_map/pallas_call | solution.py:309
  (142 shorter events, 76.5 us)
Async XLA Ops:
  23.3 14.4 %collective-permute-start.5 = (bf16[128,2304]{1,0:T(8,128)(2,1)S(1)}, bf16[128,2304]{1,0:T(8,128)(2,1)S(1)}, u32[]{:S(2)}, u32[]{:S(2)}) collective-permute-start(bf16[128,2304]{1,0:T(8,128)(2,1)S(1)} %constant_dynamic-update-slice_fusion), channel_id=1, source_target_pairs={{0,1},{1,2},{2,3},{3,0},{4,5},{5,6},{6,7},{7,4},{8,9},{9,10},{10,1... | collective-permute-start | bytes 1769480 | tf_op jit(solution)/shard_map/ppermute | solution.py:23
  24.8 12.9 %collective-permute-start.4 = (bf16[128,2304]{1,0:T(8,128)(2,1)S(1)}, bf16[128,2304]{1,0:T(8,128)(2,1)S(1)}, u32[]{:S(2)}, u32[]{:S(2)}) collective-permute-start(bf16[128,2304]{1,0:T(8,128)(2,1)S(1)} %constant_dynamic-update-slice_fusion), channel_id=1, source_target_pairs={{0,3},{1,0},{2,1},{3,2},{4,7},{5,4},{6,5},{7,6},{8,11},{9,8},{10,9... | collective-permute-start | bytes 1769480 | tf_op jit(solution)/shard_map/ppermute | solution.py:23
  37.9 13.1 %collective-permute-start.6 = (bf16[3,128,2304]{2,1,0:T(8,128)(2,1)S(1)}, bf16[3,128,2304]{2,1,0:T(8,128)(2,1)}, u32[]{:S(2)}, u32[]{:S(2)}) collective-permute-start(bf16[3,128,2304]{2,1,0:T(8,128)(2,1)S(1)} %pad_maximum_fusion.near_ref), channel_id=1, source_target_pairs={{0,16},{16,0},{1,17},{17,1},{2,18},{18,2},{3,19},{19,3},{4,20},{20... | collective-permute-start | bytes 5308424 | tf_op jit(solution)/shard_map/ppermute | solution.py:236
  65.7 12.5 %collective-permute-start.10 = (bf16[128,1536]{1,0:T(8,128)(2,1)S(1)}, bf16[128,1536]{1,0:T(8,128)(2,1)S(1)}, u32[]{:S(2)}, u32[]{:S(2)}) collective-permute-start(bf16[128,1536]{1,0:T(8,128)(2,1)S(1)} %get-tuple-element.27), channel_id=1, source_target_pairs={{0,1},{1,2},{2,3},{3,0},{4,5},{5,6},{6,7},{7,4},{8,9},{9,10},{10,1... | collective-permute-start | bytes 1179656 | tf_op jit(solution)/shard_map/ppermute | solution.py:23
  78.4 19.2 %collective-permute-start.13 = (bf16[256,1536]{1,0:T(8,128)(2,1)S(1)}, bf16[256,1536]{1,0:T(8,128)(2,1)S(1)}, u32[]{:S(2)}, u32[]{:S(2)}) collective-permute-start(bf16[256,1536]{1,0:T(8,128)(2,1)S(1)} %pad_maximum_fusion.2), channel_id=1, source_target_pairs={{0,3},{1,0},{2,1},{3,2},{4,7},{5,4},{6,5},{7,6},{8,11},{9,8},{10,9... | collective-permute-start | bytes 2359304 | tf_op jit(solution)/shard_map/ppermute | solution.py:23
  81.6 19.7 %collective-permute-start.11 = (bf16[256,1536]{1,0:T(8,128)(2,1)S(1)}, bf16[256,1536]{1,0:T(8,128)(2,1)S(1)}, u32[]{:S(2)}, u32[]{:S(2)}) collective-permute-start(bf16[256,1536]{1,0:T(8,128)(2,1)S(1)} %pad_maximum_fusion.1), channel_id=1, source_target_pairs={{0,1},{1,2},{2,3},{3,0},{4,5},{5,6},{6,7},{7,4},{8,9},{9,10},{10,1... | collective-permute-start | bytes 2359304 | tf_op jit(solution)/shard_map/ppermute | solution.py:23
  82.6 12.7 %collective-permute-start.14 = (bf16[128,768]{1,0:T(8,128)(2,1)S(1)}, bf16[128,768]{1,0:T(8,128)(2,1)S(1)}, u32[]{:S(2)}, u32[]{:S(2)}) collective-permute-start(bf16[128,768]{1,0:T(8,128)(2,1)S(1)} %bitcast.47), channel_id=1, source_target_pairs={{0,4},{4,8},{8,12},{12,0},{1,5},{5,9},{9,13},{13,1},{2,6},{6,10},{... | collective-permute-start | bytes 589832 | tf_op jit(solution)/shard_map/ppermute | solution.py:23
  86.4 21.1 %collective-permute-start.16 = (bf16[128,768]{1,0:T(8,128)(2,1)}, bf16[128,768]{1,0:T(8,128)(2,1)}, u32[]{:S(2)}, u32[]{:S(2)}) collective-permute-start(bf16[128,768]{1,0:T(8,128)(2,1)} %bitcast.22), channel_id=1, source_target_pairs={{0,12},{4,0},{8,4},{12,8},{1,13},{5,1},{9,5},{13,9},{2,14},{6,2},{... | collective-permute-start | bytes 589832 | tf_op jit(solution)/shard_map/ppermute | solution.py:23
  95.4 17.5 %collective-permute-start.15 = (bf16[256,768]{1,0:T(8,128)(2,1)S(1)}, bf16[256,768]{1,0:T(8,128)(2,1)S(1)}, u32[]{:S(2)}, u32[]{:S(2)}) collective-permute-start(bf16[256,768]{1,0:T(8,128)(2,1)S(1)} %pad_maximum_fusion.3), channel_id=1, source_target_pairs={{0,4},{4,8},{8,12},{12,0},{1,5},{5,9},{9,13},{13,1},{2,6},{6,10},{... | collective-permute-start | bytes 1179656 | tf_op jit(solution)/shard_map/ppermute | solution.py:23
  102.5 49.1 %all-to-all-start = ((bf16[4,64,1536]{2,1,0:T(8,128)(2,1)}), bf16[4,64,1536]{2,1,0:T(8,128)(2,1)S(1)}, u32[]{:S(2)}, u32[]{:S(2)}) async-start(bf16[4,64,1536]{2,1,0:T(8,128)(2,1)} %bitcast.15), calls=%async_computation | async-start | bytes 1572864 | tf_op jit(solution)/shard_map/all_to_all | solution.py:275
  108.5 34.1 %collective-permute-start.17 = (bf16[256,768]{1,0:T(8,128)(2,1)S(1)}, bf16[256,768]{1,0:T(8,128)(2,1)S(1)}, u32[]{:S(2)}, u32[]{:S(2)}) collective-permute-start(bf16[256,768]{1,0:T(8,128)(2,1)S(1)} %pad_maximum_fusion.4), channel_id=1, source_target_pairs={{0,12},{4,0},{8,4},{12,8},{1,13},{5,1},{9,5},{13,9},{2,14},{6,2},{... | collective-permute-start | bytes 1179656 | tf_op jit(solution)/shard_map/ppermute | solution.py:23
  182.6 13.6 %collective-permute-start.23 = (bf16[64,1536]{1,0:T(8,128)(2,1)}, bf16[64,1536]{1,0:T(8,128)(2,1)S(1)}, u32[]{:S(2)}, u32[]{:S(2)}) collective-permute-start(bf16[64,1536]{1,0:T(8,128)(2,1)} %get-tuple-element.15), channel_id=1, source_target_pairs={{0,4},{4,8},{8,12},{12,0},{1,5},{5,9},{9,13},{13,1},{2,6},{6,10},{... | collective-permute-start | bytes 589832 | tf_op jit(solution)/shard_map/ppermute | solution.py:23
  185.8 12.8 %collective-permute-start.21 = (bf16[64,1536]{1,0:T(8,128)(2,1)}, bf16[64,1536]{1,0:T(8,128)(2,1)S(1)}, u32[]{:S(2)}, u32[]{:S(2)}) collective-permute-start(bf16[64,1536]{1,0:T(8,128)(2,1)} %get-tuple-element.15), channel_id=1, source_target_pairs={{0,12},{4,0},{8,4},{12,8},{1,13},{5,1},{9,5},{13,9},{2,14},{6,2},{... | collective-permute-start | bytes 589832 | tf_op jit(solution)/shard_map/ppermute | solution.py:23
  205.2 29.6 %collective-permute-start.27 = (bf16[256,1536]{1,0:T(8,128)(2,1)S(1)}, bf16[256,1536]{1,0:T(8,128)(2,1)S(1)}, u32[]{:S(2)}, u32[]{:S(2)}) collective-permute-start(bf16[256,1536]{1,0:T(8,128)(2,1)S(1)} %constant_dynamic-update-slice_fusion.5.a0), channel_id=1, source_target_pairs={{0,1},{1,2},{2,3},{3,0},{4,5},{5,6},{6,7},{7,4},{8,9},{9,10},{10,1... | collective-permute-start | bytes 2359304 | tf_op jit(solution)/shard_map/ppermute | solution.py:23
  205.3 29.6 %collective-permute-start.25 = (bf16[256,1536]{1,0:T(8,128)(2,1)S(1)}, bf16[256,1536]{1,0:T(8,128)(2,1)S(1)}, u32[]{:S(2)}, u32[]{:S(2)}) collective-permute-start(bf16[256,1536]{1,0:T(8,128)(2,1)S(1)} %constant_dynamic-update-slice_fusion.5.a0), channel_id=1, source_target_pairs={{0,3},{1,0},{2,1},{3,2},{4,7},{5,4},{6,5},{7,6},{8,11},{9,8},{10,9... | collective-permute-start | bytes 2359304 | tf_op jit(solution)/shard_map/ppermute | solution.py:23
  208.5 22.0 %collective-permute-start.31 = (bf16[64,896]{1,0:T(8,128)(2,1)S(1)}, bf16[64,896]{1,0:T(8,128)(2,1)S(1)}, u32[]{:S(2)}, u32[]{:S(2)}) collective-permute-start(bf16[64,896]{1,0:T(8,128)(2,1)S(1)} %copy-done.17), channel_id=1, source_target_pairs={{0,1},{1,2},{2,3},{3,0},{4,5},{5,6},{6,7},{7,4},{8,9},{9,10},{10,1... | collective-permute-start | bytes 344072 | tf_op jit(solution)/shard_map/ppermute | solution.py:23
  208.5 21.3 %collective-permute-start.30 = (bf16[64,896]{1,0:T(8,128)(2,1)S(1)}, bf16[64,896]{1,0:T(8,128)(2,1)S(1)}, u32[]{:S(2)}, u32[]{:S(2)}) collective-permute-start(bf16[64,896]{1,0:T(8,128)(2,1)S(1)} %copy-done.17), channel_id=1, source_target_pairs={{0,2},{1,3},{2,0},{3,1},{4,6},{5,7},{6,4},{7,5},{8,10},{9,11},{10,... | collective-permute-start | bytes 344072 | tf_op jit(solution)/shard_map/ppermute | solution.py:23
  209.9 19.8 %collective-permute-start.29 = (bf16[64,896]{1,0:T(8,128)(2,1)S(1)}, bf16[64,896]{1,0:T(8,128)(2,1)S(1)}, u32[]{:S(2)}, u32[]{:S(2)}) collective-permute-start(bf16[64,896]{1,0:T(8,128)(2,1)S(1)} %copy-done.17), channel_id=1, source_target_pairs={{0,3},{1,0},{2,1},{3,2},{4,7},{5,4},{6,5},{7,6},{8,11},{9,8},{10,9... | collective-permute-start | bytes 344072 | tf_op jit(solution)/shard_map/ppermute | solution.py:23
  230.5 23.3 %collective-permute-start.34 = (bf16[256,896]{1,0:T(8,128)(2,1)S(1)}, bf16[256,896]{1,0:T(8,128)(2,1)S(1)}, u32[]{:S(2)}, u32[]{:S(2)}) collective-permute-start(bf16[256,896]{1,0:T(8,128)(2,1)S(1)} %constant_dynamic-update-slice_fusion.10.b0), channel_id=1, source_target_pairs={{0,4},{4,8},{8,12},{12,0},{1,5},{5,9},{9,13},{13,1},{2,6},{6,10},{... | collective-permute-start | bytes 1376264 | tf_op jit(solution)/shard_map/ppermute | solution.py:23
  231.5 22.4 %collective-permute-start.32 = (bf16[256,896]{1,0:T(8,128)(2,1)S(1)}, bf16[256,896]{1,0:T(8,128)(2,1)S(1)}, u32[]{:S(2)}, u32[]{:S(2)}) collective-permute-start(bf16[256,896]{1,0:T(8,128)(2,1)S(1)} %constant_dynamic-update-slice_fusion.10.b0), channel_id=1, source_target_pairs={{0,12},{4,0},{8,4},{12,8},{1,13},{5,1},{9,5},{13,9},{2,14},{6,2},{... | collective-permute-start | bytes 1376264 | tf_op jit(solution)/shard_map/ppermute | solution.py:23
  234.8 31.7 %collective-permute-start.28 = (bf16[128,1536]{1,0:T(8,128)(2,1)S(1)}, bf16[128,1536]{1,0:T(8,128)(2,1)S(1)}, u32[]{:S(2)}, u32[]{:S(2)}) collective-permute-start(bf16[128,1536]{1,0:T(8,128)(2,1)S(1)} %slice.171), channel_id=1, source_target_pairs={{0,1},{1,2},{2,3},{3,0},{4,5},{5,6},{6,7},{7,4},{8,9},{9,10},{10,1... | collective-permute-start | bytes 1179656 | tf_op jit(solution)/shard_map/ppermute | solution.py:23
  234.9 31.6 %collective-permute-start.26 = (bf16[128,1536]{1,0:T(8,128)(2,1)S(1)}, bf16[128,1536]{1,0:T(8,128)(2,1)S(1)}, u32[]{:S(2)}, u32[]{:S(2)}) collective-permute-start(bf16[128,1536]{1,0:T(8,128)(2,1)S(1)} %slice.170), channel_id=1, source_target_pairs={{0,3},{1,0},{2,1},{3,2},{4,7},{5,4},{6,5},{7,6},{8,11},{9,8},{10,9... | collective-permute-start | bytes 1179656 | tf_op jit(solution)/shard_map/ppermute | solution.py:23
  253.9 12.6 %collective-permute-start.35 = (bf16[128,896]{1,0:T(8,128)(2,1)S(1)}, bf16[128,896]{1,0:T(8,128)(2,1)S(1)}, u32[]{:S(2)}, u32[]{:S(2)}) collective-permute-start(bf16[128,896]{1,0:T(8,128)(2,1)S(1)} %slice.173), channel_id=1, source_target_pairs={{0,4},{4,8},{8,12},{12,0},{1,5},{5,9},{9,13},{13,1},{2,6},{6,10},{... | collective-permute-start | bytes 688136 | tf_op jit(solution)/shard_map/ppermute | solution.py:23
  254.0 12.5 %collective-permute-start.33 = (bf16[128,896]{1,0:T(8,128)(2,1)S(1)}, bf16[128,896]{1,0:T(8,128)(2,1)S(1)}, u32[]{:S(2)}, u32[]{:S(2)}) collective-permute-start(bf16[128,896]{1,0:T(8,128)(2,1)S(1)} %slice.172), channel_id=1, source_target_pairs={{0,12},{4,0},{8,4},{12,8},{1,13},{5,1},{9,5},{13,9},{2,14},{6,2},{... | collective-permute-start | bytes 688136 | tf_op jit(solution)/shard_map/ppermute | solution.py:23
  (35 other events, 370.0 us)

commit v3 on v2

--- a/solution.py
+++ b/solution.py
@@ -14,7 +14,7 @@
 N = 4
 BANDS = 16
 LANES = 128
-DOWN = 1536
+DOWN = 1408
 UP = 1536
 Shape = jax.ShapeDtypeStruct
 
@@ -76,7 +76,7 @@
 
 def backward_kernel(
     a0, a1, a2, a3, a4, b0, b1, b2, b3, b4, dec_any, linear_any, active_any, gathered_any,
-    enc_out, dec_out, found_ref, up_ref, extra_ref, grad_ref, dec_ref, linear_ref, active_ref, gathered_ref, sems, up_sems,
+    enc_out, dec_out, found_ref, up_ref, extra_ref, grad_ref, dec_ref, linear_ref, active_ref, gathered_ref, turned_ref, sems, up_sems,
 ):
     block = a0.shape[0]
     rows = block // N
@@ -113,17 +113,17 @@
     def first(x, _):
         for k in range(N):
 
-            @pl.when(x == k)
+            @pl.when(x == k // 2)
             def _():
                 for copy in parts[k]:
                     copy.wait()
 
-        span = pl.ds(pl.multiple_of(block * x, block), block)
+        span = pl.ds(pl.multiple_of(2 * block * x, 2 * block), 2 * block)
         grads = lax.dot_general(up_ref[span], dec_ref[...], (((1,), (1,)), ((), ())), preferred_element_type=F32)
         grad_ref[span] = (2.0 * linear_ref[span] * grads).astype(BF)
         return 0
 
-    lax.fori_loop(0, N, first, 0)
+    lax.fori_loop(0, N // 2, first, 0)
     found = jnp.zeros((8, LANES), F32)
     for i in range(N * N):
         found = found + extra_ref[rows * i : rows * i + 8].astype(F32)
@@ -133,24 +133,25 @@
     step = 2 * LANES
     whole[2].wait()
 
+    turned_ref[...] = active_ref[...].T
+
     def second(i, _):
         span = pl.ds(pl.multiple_of(step * i, step), step)
-        dec_out[span] = lax.dot_general(
-            active_ref[:, span], up_ref[...], contract, preferred_element_type=F32
-        ).astype(BF)
+        dec_out[:, span] = jnp.dot(turned_ref[...], up_ref[:, span], preferred_element_type=F32).astype(BF)
         return 0
 
-    lax.fori_loop(0, active_ref.shape[1] // step, second, 0)
+    lax.fori_loop(0, width // step, second, 0)
+    tall = 3 * step
     whole[3].wait()
 
     def third(i, _):
-        span = pl.ds(pl.multiple_of(step * i, step), step)
+        span = pl.ds(pl.multiple_of(tall * i, tall), tall)
         enc_out[span] = lax.dot_general(
             gathered_ref[:, span], grad_ref[...], contract, preferred_element_type=F32
         ).astype(BF)
         return 0
 
-    lax.fori_loop(0, width // step, third, 0)
+    lax.fori_loop(0, width // tall, third, 0)
 
 
 def deal_kernel(core_ref, a_ref, b0, b1, b2, b3, dealt_ref):
@@ -319,6 +320,7 @@
             pltpu.VMEM((total, latents), F32),
             pltpu.VMEM((total, latents), BF),
             pltpu.VMEM((total, width), BF),
+            pltpu.VMEM((latents, total), BF),
             pltpu.SemaphoreType.DMA((4,)),
             pltpu.SemaphoreType.DMA((N, 2 + 2 * N)),
         ],

time: 286 us -> 262 us (0.916)
  the two profiles are of different devices: /device:TPU:8 before, /device:TPU:48 now
where the time goes in v3:
time: 262 us; the launch traced here: 261 us
  waiting for transfers between devices  122 us (47%)
  starting transfers between devices  75.9 us (29%)
  Pallas kernels  33.9 us (13%)
  blocking collectives  12.9 us (5%)
  local copies, waits for them, and re-layouts  9.92 us (4%)
  other arithmetic  5.42 us (2%)
    ppermute x34, waiting for transfers between devices, pull(): return lax.ppermute(value, axis, [(i, (i - step) % N) for i in range(N)])  116 us
    ppermute x34, starting transfers between devices, pull(): return lax.ppermute(value, axis, [(i, (i - step) % N) for i in range(N)])  64.4 us
    pallas_call x1, Pallas kernels, step(): pl.pallas_call(backward_kernel, in_specs=[anywhere] * 14, out_specs=[LOCA...  15.9 us
    all_to_all x1, blocking collectives, step(): ups = lax.all_to_all(ups, BAND, 0, 0)  12.9 us
    pallas_call x1, Pallas kernels, step(): pl.pallas_call(forward_kernel, grid_spec=pltpu.PrefetchScalarGridSpec(num...  12.3 us
    unnamed x53, local copies, waits for them, and re-layouts  5.95 us
    all_to_all x1, starting transfers between devices, step(): mixed = lax.all_to_all(dealt, BAND, 0, 0)  5.72 us
    all_to_all x1, starting transfers between devices, step(): first = lax.all_to_all(first.reshape(N, rows, DOWN), 'zh', 0, 0)  5.56 us
  transfers between devices with their start and end apart: 38, of which 24 were waited for; matrix products, arithmetic and copies ran while one was open for 3% of the time, Pallas kernels for 0%

profile of v3, /device:TPU:48, one launch (start us, length us, event | category | flops | bytes accessed | tf_op | source)
XLA Modules:
  0.0 261.1 jit_solution(12028596681763969149)
XLA Ops:
  7.1 6.9 %collective-permute-done.2 = bf16[32,2304]{1,0:T(8,128)(2,1)S(1)} collective-permute-done((bf16[32,2304]{1,0:T(8,128)(2,1)S(1)}, bf16[32,2304]{1,0:T(8,128)(2,1)S(1)}, u32[]{:S(2)}, u32[]{:S(2)}) %collective-permute-start.2) | collective-permute-done | bytes 147488 | tf_op jit(solution)/shard_map/ppermute | solution.py:23
  14.2 4.1 %collective-permute-start.1 = (bf16[16,2304]{1,0:T(8,128)(2,1)S(1)}, bf16[16,2304]{1,0:T(8,128)(2,1)S(1)}, u32[]{:S(2)}, u32[]{:S(2)}) collective-permute-start(bf16[16,2304]{1,0:T(8,128)(2,1)S(1)} %slice.160), channel_id=1, source_target_pairs={{0,12},{4,0},{8,4},{12,8},{1,13},{5,1},{9,5},{13,9},{2,14},{6,2},{... | collective-permute-start | bytes 221192 | tf_op jit(solution)/shard_map/ppermute | solution.py:23
  24.4 11.6 %collective-permute-done.5 = bf16[128,2304]{1,0:T(8,128)(2,1)S(1)} collective-permute-done((bf16[128,2304]{1,0:T(8,128)(2,1)S(1)}, bf16[128,2304]{1,0:T(8,128)(2,1)S(1)}, u32[]{:S(2)}, u32[]{:S(2)}) %collective-permute-start.5) | collective-permute-done | bytes 589856 | tf_op jit(solution)/shard_map/ppermute | solution.py:23
  39.7 7.3 %collective-permute-done.8 = bf16[64,2304]{1,0:T(8,128)(2,1)S(1)} collective-permute-done((bf16[64,2304]{1,0:T(8,128)(2,1)S(1)}, bf16[64,2304]{1,0:T(8,128)(2,1)S(1)}, u32[]{:S(2)}, u32[]{:S(2)}) %collective-permute-start.8) | collective-permute-done | bytes 294944 | tf_op jit(solution)/shard_map/ppermute | solution.py:23
  50.0 12.3 %shard_map.67 = (bf16[1024,2304]{1,0:T(8,128)(2,1)}, f32[1024,512]{1,0:T(8,128)}, bf16[1024,512]{1,0:T(8,128)(2,1)}, bf16[4,256,1408]{2,1,0:T(8,128)(2,1)}, bf16[4,4,64,896]{3,2,1,0:T(8,128)(2,1)}) custom-call(s32[2]{0:T(128)} %pad_add_fusion.at_ref, bf16[3,128,2304]{2,1,0:T(8,128)(2,1)} %copy-done, bf16[3,128,2304]{2,1,0:T(8,128)(2,1)} %collective-permute-done.6.near2_ref, ...), custom_call_target="tpu_custom_call" | custom-call | tf_op jit(solution)/shard_map/pallas_call | solution.py:243
  67.3 4.4 %collective-permute-start.16 = (bf16[128,896]{1,0:T(8,128)(2,1)S(1)}, bf16[128,896]{1,0:T(8,128)(2,1)S(1)}, u32[]{:S(2)}, u32[]{:S(2)}) collective-permute-start(bf16[128,896]{1,0:T(8,128)(2,1)S(1)} %bitcast.47), channel_id=1, source_target_pairs={{0,12},{4,0},{8,4},{12,8},{1,13},{5,1},{9,5},{13,9},{2,14},{6,2},{... | collective-permute-start | bytes 688136 | tf_op jit(solution)/shard_map/ppermute | solution.py:23
  71.7 3.9 %collective-permute-done.10 = bf16[128,1408]{1,0:T(8,128)(2,1)S(1)} collective-permute-done((bf16[128,1408]{1,0:T(8,128)(2,1)S(1)}, bf16[128,1408]{1,0:T(8,128)(2,1)S(1)}, u32[]{:S(2)}, u32[]{:S(2)}) %collective-permute-start.10) | collective-permute-done | bytes 360480 | tf_op jit(solution)/shard_map/ppermute | solution.py:23
  79.2 6.5 %collective-permute-done.14 = bf16[128,896]{1,0:T(8,128)(2,1)S(1)} collective-permute-done((bf16[128,896]{1,0:T(8,128)(2,1)S(1)}, bf16[128,896]{1,0:T(8,128)(2,1)S(1)}, u32[]{:S(2)}, u32[]{:S(2)}) %collective-permute-start.14) | collective-permute-done | bytes 229408 | tf_op jit(solution)/shard_map/ppermute | solution.py:23
  87.5 4.1 %collective-permute-start.17 = (bf16[256,896]{1,0:T(8,128)(2,1)}, bf16[256,896]{1,0:T(8,128)(2,1)S(1)}, u32[]{:S(2)}, u32[]{:S(2)}) collective-permute-start(bf16[256,896]{1,0:T(8,128)(2,1)} %pad_maximum_fusion.4), channel_id=1, source_target_pairs={{0,12},{4,0},{8,4},{12,8},{1,13},{5,1},{9,5},{13,9},{2,14},{6,2},{... | collective-permute-start | bytes 1376264 | tf_op jit(solution)/shard_map/ppermute | solution.py:23
  93.7 3.6 %collective-permute-done.11 = bf16[256,1408]{1,0:T(8,128)(2,1)S(1)} collective-permute-done((bf16[256,1408]{1,0:T(8,128)(2,1)S(1)}, bf16[256,1408]{1,0:T(8,128)(2,1)S(1)}, u32[]{:S(2)}, u32[]{:S(2)}) %collective-permute-start.11) | collective-permute-done | bytes 720928 | tf_op jit(solution)/shard_map/ppermute | solution.py:23
  98.4 5.6 %all-to-all-start = ((bf16[4,64,1408]{2,1,0:T(8,128)(2,1)}), bf16[4,64,1408]{2,1,0:T(8,128)(2,1)S(1)}, u32[]{:S(2)}, u32[]{:S(2)}) async-start(bf16[4,64,1408]{2,1,0:T(8,128)(2,1)} %bitcast.15), calls=%async_computation | async-start | bytes 1441792 | tf_op jit(solution)/shard_map/all_to_all | solution.py:276
  104.0 10.7 %collective-permute-done.15 = bf16[256,896]{1,0:T(8,128)(2,1)S(1)} collective-permute-done((bf16[256,896]{1,0:T(8,128)(2,1)}, bf16[256,896]{1,0:T(8,128)(2,1)S(1)}, u32[]{:S(2)}, u32[]{:S(2)}) %collective-permute-start.15) | collective-permute-done | bytes 458784 | tf_op jit(solution)/shard_map/ppermute | solution.py:23
  128.9 5.7 %all-to-all-start.1 = ((bf16[16,8,1152]{2,1,0:T(8,128)(2,1)}), bf16[16,8,1152]{2,1,0:T(8,128)(2,1)S(1)}, u32[]{:S(2)}, u32[]{:S(2)}) async-start(bf16[16,8,1152]{2,1,0:T(8,128)(2,1)} %shard_map.68), calls=%async_computation.1 | async-start | bytes 589824 | tf_op jit(solution)/shard_map/all_to_all | solution.py:287
  136.0 3.6 %all-to-all-done.1.mixed_ref = bf16[16,8,1152]{2,1,0:T(8,128)(2,1)S(1)} async-done(((bf16[16,8,1152]{2,1,0:T(8,128)(2,1)}), bf16[16,8,1152]{2,1,0:T(8,128)(2,1)S(1)}, u32[]{:S(2)}, u32[]{:S(2)}) %all-to-all-start.1) | async-done | bytes 294944 | tf_op jit(solution)/shard_map/all_to_all | solution.py:287
  142.2 12.9 %all_to_all.15.mixed_ref = bf16[16,8,1280]{2,1,0:T(8,128)(2,1)} all-to-all(bf16[16,8,1280]{2,1,0:T(8,128)(2,1)} %shard_map.69), channel_id=1, replica_groups=mesh['y'=4,'zl'=2,'core'=2,'zh'=4,'x'=4] {'y','zl','core'}, dimensions={0} | all-to-all | bytes 655360 | tf_op jit(solution)/shard_map/all_to_all | solution.py:295
  156.8 4.0 %collective-permute-start.23 = (bf16[64,1536]{1,0:T(8,128)(2,1)}, bf16[64,1536]{1,0:T(8,128)(2,1)S(1)}, u32[]{:S(2)}, u32[]{:S(2)}) collective-permute-start(bf16[64,1536]{1,0:T(8,128)(2,1)} %get-tuple-element.15), channel_id=1, source_target_pairs={{0,4},{4,8},{8,12},{12,0},{1,5},{5,9},{9,13},{13,1},{2,6},{6,10},{... | collective-permute-start | bytes 589832 | tf_op jit(solution)/shard_map/ppermute | solution.py:23
  161.9 8.8 %collective-permute-done.23 = bf16[64,1536]{1,0:T(8,128)(2,1)S(1)} collective-permute-done((bf16[64,1536]{1,0:T(8,128)(2,1)}, bf16[64,1536]{1,0:T(8,128)(2,1)S(1)}, u32[]{:S(2)}, u32[]{:S(2)}) %collective-permute-start.23) | collective-permute-done | bytes 196640 | tf_op jit(solution)/shard_map/ppermute | solution.py:23
  175.0 4.8 %collective-permute-done.22 = bf16[32,1536]{1,0:T(8,128)(2,1)S(1)} collective-permute-done((bf16[32,1536]{1,0:T(8,128)(2,1)S(1)}, bf16[32,1536]{1,0:T(8,128)(2,1)S(1)}, u32[]{:S(2)}, u32[]{:S(2)}) %collective-permute-start.22) | collective-permute-done | bytes 98336 | tf_op jit(solution)/shard_map/ppermute | solution.py:23
  186.5 15.8 %collective-permute-done.29 = bf16[64,896]{1,0:T(8,128)(2,1)S(1)} collective-permute-done((bf16[64,896]{1,0:T(8,128)(2,1)S(1)}, bf16[64,896]{1,0:T(8,128)(2,1)S(1)}, u32[]{:S(2)}, u32[]{:S(2)}) %collective-permute-start.29) | collective-permute-done | bytes 114720 | tf_op jit(solution)/shard_map/ppermute | solution.py:23
  203.0 5.4 %collective-permute-start.34 = (bf16[256,896]{1,0:T(8,128)(2,1)S(1)}, bf16[256,896]{1,0:T(8,128)(2,1)S(1)}, u32[]{:S(2)}, u32[]{:S(2)}) collective-permute-start(bf16[256,896]{1,0:T(8,128)(2,1)S(1)} %constant_dynamic-update-slice_fusion.10.b0), channel_id=1, source_target_pairs={{0,4},{4,8},{8,12},{12,0},{1,5},{5,9},{9,13},{13,1},{2,6},{6,10},{... | collective-permute-start | bytes 1376264 | tf_op jit(solution)/shard_map/ppermute | solution.py:23
  211.9 18.0 %collective-permute-done.34.b4 = bf16[256,896]{1,0:T(8,128)(2,1)S(1)} collective-permute-done((bf16[256,896]{1,0:T(8,128)(2,1)S(1)}, bf16[256,896]{1,0:T(8,128)(2,1)S(1)}, u32[]{:S(2)}, u32[]{:S(2)}) %collective-permute-start.34) | collective-permute-done | bytes 458784 | tf_op jit(solution)/shard_map/ppermute | solution.py:23
  229.9 5.5 %collective-permute-start.35 = (bf16[128,896]{1,0:T(8,128)(2,1)S(1)}, bf16[128,896]{1,0:T(8,128)(2,1)S(1)}, u32[]{:S(2)}, u32[]{:S(2)}) collective-permute-start(bf16[128,896]{1,0:T(8,128)(2,1)S(1)} %slice.173), channel_id=1, source_target_pairs={{0,4},{4,8},{8,12},{12,0},{1,5},{5,9},{9,13},{13,1},{2,6},{6,10},{... | collective-permute-start | bytes 688136 | tf_op jit(solution)/shard_map/ppermute | solution.py:23
  239.0 3.5 %collective-permute-done.33.b2 = bf16[128,896]{1,0:T(8,128)(2,1)S(1)} collective-permute-done((bf16[128,896]{1,0:T(8,128)(2,1)S(1)}, bf16[128,896]{1,0:T(8,128)(2,1)S(1)}, u32[]{:S(2)}, u32[]{:S(2)}) %collective-permute-start.33) | collective-permute-done | bytes 229408 | tf_op jit(solution)/shard_map/ppermute | solution.py:23
  244.0 15.9 %shard_map.71 = (bf16[2304,512]{1,0:T(8,128)(2,1)}, bf16[512,2304]{1,0:T(8,128)(2,1)}, f32[1,128]{1,0:T(1,128)}) custom-call(bf16[256,1536]{1,0:T(8,128)(2,1)} %copy-done.7, bf16[256,1536]{1,0:T(8,128)(2,1)} %copy-done.6, bf16[128,1536]{1,0:T(8,128)(2,1)} %copy-done.14, bf16[128,1536]{1,0:T(8,128)(2,1)} %copy-done.13, bf16[256,1536]{1,0:T(8,128)(2,1)} %copy-done.5, ...), custom_call_target="tpu_custom_call" | custom-call | tf_op jit(solution)/shard_map/pallas_call | solution.py:310
  (142 shorter events, 75.5 us)
Async XLA Ops:
  1.6 12.5 %collective-permute-start.2 = (bf16[32,2304]{1,0:T(8,128)(2,1)S(1)}, bf16[32,2304]{1,0:T(8,128)(2,1)S(1)}, u32[]{:S(2)}, u32[]{:S(2)}) collective-permute-start(bf16[32,2304]{1,0:T(8,128)(2,1)S(1)} %get-tuple-element.24), channel_id=1, source_target_pairs={{0,4},{4,8},{8,12},{12,0},{1,5},{5,9},{9,13},{13,1},{2,6},{6,10},{... | collective-permute-start | bytes 442376 | tf_op jit(solution)/shard_map/ppermute | solution.py:23
  21.1 14.9 %collective-permute-start.5 = (bf16[128,2304]{1,0:T(8,128)(2,1)S(1)}, bf16[128,2304]{1,0:T(8,128)(2,1)S(1)}, u32[]{:S(2)}, u32[]{:S(2)}) collective-permute-start(bf16[128,2304]{1,0:T(8,128)(2,1)S(1)} %constant_dynamic-update-slice_fusion), channel_id=1, source_target_pairs={{0,1},{1,2},{2,3},{3,0},{4,5},{5,6},{6,7},{7,4},{8,9},{9,10},{10,1... | collective-permute-start | bytes 1769480 | tf_op jit(solution)/shard_map/ppermute | solution.py:23
  22.7 13.3 %collective-permute-start.4 = (bf16[128,2304]{1,0:T(8,128)(2,1)S(1)}, bf16[128,2304]{1,0:T(8,128)(2,1)S(1)}, u32[]{:S(2)}, u32[]{:S(2)}) collective-permute-start(bf16[128,2304]{1,0:T(8,128)(2,1)S(1)} %constant_dynamic-update-slice_fusion), channel_id=1, source_target_pairs={{0,3},{1,0},{2,1},{3,2},{4,7},{5,4},{6,5},{7,6},{8,11},{9,8},{10,9... | collective-permute-start | bytes 1769480 | tf_op jit(solution)/shard_map/ppermute | solution.py:23
  36.2 13.1 %collective-permute-start.6 = (bf16[3,128,2304]{2,1,0:T(8,128)(2,1)S(1)}, bf16[3,128,2304]{2,1,0:T(8,128)(2,1)}, u32[]{:S(2)}, u32[]{:S(2)}) collective-permute-start(bf16[3,128,2304]{2,1,0:T(8,128)(2,1)S(1)} %pad_maximum_fusion.near_ref), channel_id=1, source_target_pairs={{0,16},{16,0},{1,17},{17,1},{2,18},{18,2},{3,19},{19,3},{4,20},{20... | collective-permute-start | bytes 5308424 | tf_op jit(solution)/shard_map/ppermute | solution.py:237
  36.3 10.7 %collective-permute-start.8 = (bf16[64,2304]{1,0:T(8,128)(2,1)S(1)}, bf16[64,2304]{1,0:T(8,128)(2,1)S(1)}, u32[]{:S(2)}, u32[]{:S(2)}) collective-permute-start(bf16[64,2304]{1,0:T(8,128)(2,1)S(1)} %slice.163), channel_id=1, source_target_pairs={{0,1},{1,2},{2,3},{3,0},{4,5},{5,6},{6,7},{7,4},{8,9},{9,10},{10,1... | collective-permute-start | bytes 884744 | tf_op jit(solution)/shard_map/ppermute | solution.py:23
  63.9 11.8 %collective-permute-start.10 = (bf16[128,1408]{1,0:T(8,128)(2,1)S(1)}, bf16[128,1408]{1,0:T(8,128)(2,1)S(1)}, u32[]{:S(2)}, u32[]{:S(2)}) collective-permute-start(bf16[128,1408]{1,0:T(8,128)(2,1)S(1)} %get-tuple-element.27), channel_id=1, source_target_pairs={{0,1},{1,2},{2,3},{3,0},{4,5},{5,6},{6,7},{7,4},{8,9},{9,10},{10,1... | collective-permute-start | bytes 1081352 | tf_op jit(solution)/shard_map/ppermute | solution.py:23
  67.3 19.2 %collective-permute-start.16 = (bf16[128,896]{1,0:T(8,128)(2,1)S(1)}, bf16[128,896]{1,0:T(8,128)(2,1)S(1)}, u32[]{:S(2)}, u32[]{:S(2)}) collective-permute-start(bf16[128,896]{1,0:T(8,128)(2,1)S(1)} %bitcast.47), channel_id=1, source_target_pairs={{0,12},{4,0},{8,4},{12,8},{1,13},{5,1},{9,5},{13,9},{2,14},{6,2},{... | collective-permute-start | bytes 688136 | tf_op jit(solution)/shard_map/ppermute | solution.py:23
  71.7 13.9 %collective-permute-start.14 = (bf16[128,896]{1,0:T(8,128)(2,1)S(1)}, bf16[128,896]{1,0:T(8,128)(2,1)S(1)}, u32[]{:S(2)}, u32[]{:S(2)}) collective-permute-start(bf16[128,896]{1,0:T(8,128)(2,1)S(1)} %bitcast.48), channel_id=1, source_target_pairs={{0,4},{4,8},{8,12},{12,0},{1,5},{5,9},{9,13},{13,1},{2,6},{6,10},{... | collective-permute-start | bytes 688136 | tf_op jit(solution)/shard_map/ppermute | solution.py:23
  75.9 17.8 %collective-permute-start.13 = (bf16[256,1408]{1,0:T(8,128)(2,1)S(1)}, bf16[256,1408]{1,0:T(8,128)(2,1)S(1)}, u32[]{:S(2)}, u32[]{:S(2)}) collective-permute-start(bf16[256,1408]{1,0:T(8,128)(2,1)S(1)} %pad_maximum_fusion.2), channel_id=1, source_target_pairs={{0,3},{1,0},{2,1},{3,2},{4,7},{5,4},{6,5},{7,6},{8,11},{9,8},{10,9... | collective-permute-start | bytes 2162696 | tf_op jit(solution)/shard_map/ppermute | solution.py:23
  79.1 18.2 %collective-permute-start.11 = (bf16[256,1408]{1,0:T(8,128)(2,1)S(1)}, bf16[256,1408]{1,0:T(8,128)(2,1)S(1)}, u32[]{:S(2)}, u32[]{:S(2)}) collective-permute-start(bf16[256,1408]{1,0:T(8,128)(2,1)S(1)} %pad_maximum_fusion.1), channel_id=1, source_target_pairs={{0,1},{1,2},{2,3},{3,0},{4,5},{5,6},{6,7},{7,4},{8,9},{9,10},{10,1... | collective-permute-start | bytes 2162696 | tf_op jit(solution)/shard_map/ppermute | solution.py:23
  86.6 28.1 %collective-permute-start.15 = (bf16[256,896]{1,0:T(8,128)(2,1)}, bf16[256,896]{1,0:T(8,128)(2,1)S(1)}, u32[]{:S(2)}, u32[]{:S(2)}) collective-permute-start(bf16[256,896]{1,0:T(8,128)(2,1)} %pad_maximum_fusion.3), channel_id=1, source_target_pairs={{0,4},{4,8},{8,12},{12,0},{1,5},{5,9},{9,13},{13,1},{2,6},{6,10},{... | collective-permute-start | bytes 1376264 | tf_op jit(solution)/shard_map/ppermute | solution.py:23
  87.5 27.2 %collective-permute-start.17 = (bf16[256,896]{1,0:T(8,128)(2,1)}, bf16[256,896]{1,0:T(8,128)(2,1)S(1)}, u32[]{:S(2)}, u32[]{:S(2)}) collective-permute-start(bf16[256,896]{1,0:T(8,128)(2,1)} %pad_maximum_fusion.4), channel_id=1, source_target_pairs={{0,12},{4,0},{8,4},{12,8},{1,13},{5,1},{9,5},{13,9},{2,14},{6,2},{... | collective-permute-start | bytes 1376264 | tf_op jit(solution)/shard_map/ppermute | solution.py:23
  98.4 27.6 %all-to-all-start = ((bf16[4,64,1408]{2,1,0:T(8,128)(2,1)}), bf16[4,64,1408]{2,1,0:T(8,128)(2,1)S(1)}, u32[]{:S(2)}, u32[]{:S(2)}) async-start(bf16[4,64,1408]{2,1,0:T(8,128)(2,1)} %bitcast.15), calls=%async_computation | async-start | bytes 1441792 | tf_op jit(solution)/shard_map/all_to_all | solution.py:276
  156.8 13.9 %collective-permute-start.23 = (bf16[64,1536]{1,0:T(8,128)(2,1)}, bf16[64,1536]{1,0:T(8,128)(2,1)S(1)}, u32[]{:S(2)}, u32[]{:S(2)}) collective-permute-start(bf16[64,1536]{1,0:T(8,128)(2,1)} %get-tuple-element.15), channel_id=1, source_target_pairs={{0,4},{4,8},{8,12},{12,0},{1,5},{5,9},{9,13},{13,1},{2,6},{6,10},{... | collective-permute-start | bytes 589832 | tf_op jit(solution)/shard_map/ppermute | solution.py:23
  160.7 12.4 %collective-permute-start.21 = (bf16[64,1536]{1,0:T(8,128)(2,1)}, bf16[64,1536]{1,0:T(8,128)(2,1)S(1)}, u32[]{:S(2)}, u32[]{:S(2)}) collective-permute-start(bf16[64,1536]{1,0:T(8,128)(2,1)} %get-tuple-element.15), channel_id=1, source_target_pairs={{0,12},{4,0},{8,4},{12,8},{1,13},{5,1},{9,5},{13,9},{2,14},{6,2},{... | collective-permute-start | bytes 589832 | tf_op jit(solution)/shard_map/ppermute | solution.py:23
  179.9 28.6 %collective-permute-start.27 = (bf16[256,1536]{1,0:T(8,128)(2,1)S(1)}, bf16[256,1536]{1,0:T(8,128)(2,1)S(1)}, u32[]{:S(2)}, u32[]{:S(2)}) collective-permute-start(bf16[256,1536]{1,0:T(8,128)(2,1)S(1)} %constant_dynamic-update-slice_fusion.5.a0), channel_id=1, source_target_pairs={{0,1},{1,2},{2,3},{3,0},{4,5},{5,6},{6,7},{7,4},{8,9},{9,10},{10,1... | collective-permute-start | bytes 2359304 | tf_op jit(solution)/shard_map/ppermute | solution.py:23
  180.0 28.6 %collective-permute-start.25 = (bf16[256,1536]{1,0:T(8,128)(2,1)S(1)}, bf16[256,1536]{1,0:T(8,128)(2,1)S(1)}, u32[]{:S(2)}, u32[]{:S(2)}) collective-permute-start(bf16[256,1536]{1,0:T(8,128)(2,1)S(1)} %constant_dynamic-update-slice_fusion.5.a0), channel_id=1, source_target_pairs={{0,3},{1,0},{2,1},{3,2},{4,7},{5,4},{6,5},{7,6},{8,11},{9,8},{10,9... | collective-permute-start | bytes 2359304 | tf_op jit(solution)/shard_map/ppermute | solution.py:23
  183.2 19.8 %collective-permute-start.31 = (bf16[64,896]{1,0:T(8,128)(2,1)S(1)}, bf16[64,896]{1,0:T(8,128)(2,1)S(1)}, u32[]{:S(2)}, u32[]{:S(2)}) collective-permute-start(bf16[64,896]{1,0:T(8,128)(2,1)S(1)} %copy-done.17), channel_id=1, source_target_pairs={{0,1},{1,2},{2,3},{3,0},{4,5},{5,6},{6,7},{7,4},{8,9},{9,10},{10,1... | collective-permute-start | bytes 344072 | tf_op jit(solution)/shard_map/ppermute | solution.py:23
  183.2 19.2 %collective-permute-start.30 = (bf16[64,896]{1,0:T(8,128)(2,1)S(1)}, bf16[64,896]{1,0:T(8,128)(2,1)S(1)}, u32[]{:S(2)}, u32[]{:S(2)}) collective-permute-start(bf16[64,896]{1,0:T(8,128)(2,1)S(1)} %copy-done.17), channel_id=1, source_target_pairs={{0,2},{1,3},{2,0},{3,1},{4,6},{5,7},{6,4},{7,5},{8,10},{9,11},{10,... | collective-permute-start | bytes 344072 | tf_op jit(solution)/shard_map/ppermute | solution.py:23
  184.7 17.6 %collective-permute-start.29 = (bf16[64,896]{1,0:T(8,128)(2,1)S(1)}, bf16[64,896]{1,0:T(8,128)(2,1)S(1)}, u32[]{:S(2)}, u32[]{:S(2)}) collective-permute-start(bf16[64,896]{1,0:T(8,128)(2,1)S(1)} %copy-done.17), channel_id=1, source_target_pairs={{0,3},{1,0},{2,1},{3,2},{4,7},{5,4},{6,5},{7,6},{8,11},{9,8},{10,9... | collective-permute-start | bytes 344072 | tf_op jit(solution)/shard_map/ppermute | solution.py:23
  203.0 26.9 %collective-permute-start.34 = (bf16[256,896]{1,0:T(8,128)(2,1)S(1)}, bf16[256,896]{1,0:T(8,128)(2,1)S(1)}, u32[]{:S(2)}, u32[]{:S(2)}) collective-permute-start(bf16[256,896]{1,0:T(8,128)(2,1)S(1)} %constant_dynamic-update-slice_fusion.10.b0), channel_id=1, source_target_pairs={{0,4},{4,8},{8,12},{12,0},{1,5},{5,9},{9,13},{13,1},{2,6},{6,10},{... | collective-permute-start | bytes 1376264 | tf_op jit(solution)/shard_map/ppermute | solution.py:23
  208.4 27.0 %collective-permute-start.32 = (bf16[256,896]{1,0:T(8,128)(2,1)S(1)}, bf16[256,896]{1,0:T(8,128)(2,1)S(1)}, u32[]{:S(2)}, u32[]{:S(2)}) collective-permute-start(bf16[256,896]{1,0:T(8,128)(2,1)S(1)} %constant_dynamic-update-slice_fusion.10.b0), channel_id=1, source_target_pairs={{0,12},{4,0},{8,4},{12,8},{1,13},{5,1},{9,5},{13,9},{2,14},{6,2},{... | collective-permute-start | bytes 1376264 | tf_op jit(solution)/shard_map/ppermute | solution.py:23
  208.5 34.0 %collective-permute-start.28 = (bf16[128,1536]{1,0:T(8,128)(2,1)S(1)}, bf16[128,1536]{1,0:T(8,128)(2,1)S(1)}, u32[]{:S(2)}, u32[]{:S(2)}) collective-permute-start(bf16[128,1536]{1,0:T(8,128)(2,1)S(1)} %slice.171), channel_id=1, source_target_pairs={{0,1},{1,2},{2,3},{3,0},{4,5},{5,6},{6,7},{7,4},{8,9},{9,10},{10,1... | collective-permute-start | bytes 1179656 | tf_op jit(solution)/shard_map/ppermute | solution.py:23
  208.6 33.8 %collective-permute-start.26 = (bf16[128,1536]{1,0:T(8,128)(2,1)S(1)}, bf16[128,1536]{1,0:T(8,128)(2,1)S(1)}, u32[]{:S(2)}, u32[]{:S(2)}) collective-permute-start(bf16[128,1536]{1,0:T(8,128)(2,1)S(1)} %slice.170), channel_id=1, source_target_pairs={{0,3},{1,0},{2,1},{3,2},{4,7},{5,4},{6,5},{7,6},{8,11},{9,8},{10,9... | collective-permute-start | bytes 1179656 | tf_op jit(solution)/shard_map/ppermute | solution.py:23
  (35 other events, 374.8 us)
